TPU v7x, 32 devices: a whole 2x2x4 slice. The times are simulated.
32 devices in a mesh: member: 4 (over y, x), lat: 8 (over z, core).
Axes of the slice: x: 2, y: 2, z: 4, core: 2. Of those that a mesh axis runs over, the one named last changes fastest.
Arguments:
- state: bfloat16 [4, 64, 720, 128], P('member', 'lat'), may hold values from -6 to 6
- conv_weight: bfloat16 [9, 128, 128], replicated, may hold values from -0.1875 to 0.1875
- legendre: bfloat16 [64, 64, 64], P('lat'), may hold values from -0.75 to 0.75
- quad_weight: float32 [64], replicated, may hold values from 0.5 to 2
- spectral_gain: float32 [2, 64, 128], replicated, may hold values from -4 to 4
- project_weight: float32 [128, 16], replicated, may hold values from -0.5 to 0.5
- target: bfloat16 [16, 64, 720], P(None, 'lat'), may hold values from -10 to 10
Outputs:
- field_grad: float32 [4, 16, 64, 720], P('member', None, 'lat')
All inputs are finite; a program needn't handle non-finite values.
Results may differ from a plain program's by a relative error of at most 0.0088.
Values may be sent and summed in bfloat16 or wider, within the bound.
A program may use at most 64 MiB of HBM per device.

v0:
```python
import functools
import jax
import jax.numpy as jnp
import numpy as np
from jax import lax
from jax.experimental import pallas as pl
from jax.experimental.pallas import tpu as pltpu
from jax.sharding import PartitionSpec as P


def with_halo(block, sides, width):
    for axis, dim in sides:
        count = lax.axis_size(axis)
        forward = [(i, i + 1) for i in range(count - 1)]
        backward = [(target, source) for source, target in forward]
        low = lax.ppermute(
            lax.slice_in_dim(block, block.shape[dim] - width, None, axis=dim), axis, forward
        )
        high = lax.ppermute(lax.slice_in_dim(block, 0, width, axis=dim), axis, backward)
        block = jnp.concatenate([low, block, high], axis=dim)
    return block


MESH = pl.DeviceIdType.MESH


def dft_table(nlon, modes, bands):
    phase = np.arange(nlon)[:, None] * np.arange(modes)[None, :] % nlon
    angle = phase * (2.0 * np.pi / nlon)
    table = np.stack([np.cos(angle), -np.sin(angle)], axis=1) / np.sqrt(nlon)
    table = table.reshape(nlon, 2, bands, modes // bands).swapaxes(1, 2)
    return jnp.asarray(table.reshape(nlon, 2 * modes).astype(np.float32), jnp.bfloat16)


def spread_kernel(members, bands, spec, direct, banded, everyone, sems):
    member, band = lax.axis_index("member"), lax.axis_index("lat")
    barrier = pltpu.get_barrier_semaphore()

    @pl.loop(1, bands)
    def _(k):
        pl.semaphore_signal(barrier, 1, device_id=(member, (band + k) % bands), device_id_type=MESH)

    @pl.loop(1, members)
    def _(k):
        pl.semaphore_signal(barrier, 1, device_id=((member + k) % members, band), device_id_type=MESH)

    pl.semaphore_wait(barrier, bands + members - 2)

    @pl.loop(1, bands)
    def _(k):
        peer = (band + k) % bands
        pltpu.make_async_remote_copy(
            spec.at[:, peer], banded.at[band], sems.at[0], sems.at[1],
            device_id=(member, peer), device_id_type=MESH,
        ).start()

    @pl.loop(1, members)
    def _(k):
        peer = (member + k) % members
        pltpu.make_async_remote_copy(
            direct, everyone.at[member], sems.at[2], sems.at[3],
            device_id=(peer, band), device_id_type=MESH,
        ).start()

    pltpu.make_async_copy(spec.at[:, band], banded.at[band], sems.at[1]).start()
    pltpu.make_async_copy(direct, everyone.at[member], sems.at[3]).start()
    pltpu.make_async_copy(banded, banded, sems.at[1]).wait()
    pltpu.make_async_copy(everyone, everyone, sems.at[3]).wait()
    sent = banded.at[pl.ds(0, bands - 1)]
    pltpu.make_async_copy(sent, sent, sems.at[0]).wait()
    sent = everyone.at[pl.ds(0, members - 1)]
    pltpu.make_async_copy(sent, sent, sems.at[2]).wait()


def return_kernel(members, bands, narrow, everyone, sems):
    member, band = lax.axis_index("member"), lax.axis_index("lat")
    count = members * bands
    me = member * bands + band
    barrier = pltpu.get_barrier_semaphore()

    @pl.loop(1, count)
    def _(k):
        peer = (me + k) % count
        pl.semaphore_signal(barrier, 1, device_id=(peer // bands, peer % bands), device_id_type=MESH)

    pl.semaphore_wait(barrier, count - 1)

    @pl.loop(1, count)
    def _(k):
        peer = (me + k) % count
        pltpu.make_async_remote_copy(
            narrow.at[peer % bands], everyone.at[me], sems.at[0], sems.at[1],
            device_id=(peer // bands, peer % bands), device_id_type=MESH,
        ).start()

    pltpu.make_async_copy(narrow.at[band], everyone.at[me], sems.at[1]).start()
    pltpu.make_async_copy(everyone, everyone, sems.at[1]).wait()
    sent = everyone.at[pl.ds(0, count - 1)]
    pltpu.make_async_copy(sent, sent, sems.at[0]).wait()


def exchange(kernel, ident, shapes, sems, *args):
    vmem = pl.BlockSpec(memory_space=pltpu.VMEM)
    return pl.pallas_call(
        kernel,
        out_shape=[jax.ShapeDtypeStruct(shape, jnp.bfloat16) for shape in shapes],
        in_specs=[vmem] * len(args),
        out_specs=[vmem] * len(shapes),
        scratch_shapes=[pltpu.SemaphoreType.DMA((sems,))],
        compiler_params=pltpu.CompilerParams(collective_id=ident, has_side_effects=True),
    )(*args)


def smooth(diff):
    return diff / jnp.sqrt(diff * diff + 0.25)


def local(state, conv_weight, legendre, quad_weight, spectral_gain, project_weight, target):
    field = state[0]
    lat_rows, nlon, chans = field.shape
    modes = legendre.shape[1]
    padded = with_halo(field, (("lat", 0),), 4)
    conv = lax.conv_general_dilated(
        padded,
        conv_weight,
        window_strides=(1,),
        padding="VALID",
        dimension_numbers=("WNC", "WIO", "WNC"),
        preferred_element_type=jnp.float32,
    )
    mixed = (field.astype(jnp.float32) + jax.nn.silu(conv)).astype(jnp.bfloat16)
    members, bands = lax.axis_size("member"), lax.axis_size("lat")
    wide = 2 * modes // bands
    fields = project_weight.shape[1]
    high = lax.reduce_precision(project_weight, 8, 7)
    weight = jnp.concatenate([high, project_weight - high], axis=1).astype(jnp.bfloat16)
    table = dft_table(nlon, modes, bands)
    spectrum = jnp.einsum("nk,anc->akc", table, mixed, preferred_element_type=jnp.float32).astype(
        jnp.bfloat16
    )
    direct = jnp.einsum("anc,cg->gan", mixed, weight, preferred_element_type=jnp.float32)
    direct = (direct[:fields] + direct[fields:]).astype(jnp.bfloat16)
    banded, directs = exchange(
        functools.partial(spread_kernel, members, bands),
        0,
        [(bands, lat_rows, wide, chans), (members, fields * lat_rows, nlon)],
        4,
        spectrum.reshape(lat_rows, bands, wide, chans),
        direct.reshape(fields * lat_rows, nlon),
    )
    banded = banded.reshape(bands * lat_rows, 2, modes // bands, chans)
    wtable = (legendre.astype(jnp.float32) * quad_weight[None, None, :]).astype(jnp.bfloat16)
    coef = jnp.einsum("mla,armc->mlrc", wtable, banded, preferred_element_type=jnp.float32)
    gain_re = spectral_gain[0]
    gain_im = spectral_gain[1]
    real_part = coef[:, :, 0] * gain_re[None] - coef[:, :, 1] * gain_im[None]
    imag_part = coef[:, :, 0] * gain_im[None] + coef[:, :, 1] * gain_re[None]
    filtered = jnp.stack([real_part, imag_part], axis=2).astype(jnp.bfloat16)
    back = jnp.einsum(
        "mla,mlrc->armc", legendre, filtered, preferred_element_type=jnp.float32
    ).astype(jnp.bfloat16)
    both = jnp.einsum("armc,cg->armg", back, weight, preferred_element_type=jnp.float32)
    narrow = (both[..., :fields] + both[..., fields:]).astype(jnp.bfloat16)
    narrow = narrow.reshape(bands, lat_rows, wide, fields).swapaxes(1, 2)
    (spectra,) = exchange(
        functools.partial(return_kernel, members, bands),
        1,
        [(members * bands, wide, lat_rows * fields)],
        2,
        narrow.reshape(bands, wide, lat_rows * fields),
    )
    synth = jnp.einsum(
        "jkaf,nk->jfan",
        spectra.reshape(members, 2 * modes, lat_rows, fields),
        table,
        preferred_element_type=jnp.float32,
    )
    directs = directs.reshape(members, fields, lat_rows, nlon).astype(jnp.float32)
    projected = lax.reduce_precision(directs + synth, 8, 7)
    own = lax.dynamic_index_in_dim(projected, lax.axis_index("member"), 0, keepdims=False)
    pair = jnp.sum(smooth(own[None] - projected), axis=0)
    grads = smooth(own - target.astype(jnp.float32)) - pair / (members - 1)
    return grads[None]


def solution(mesh):
    return jax.shard_map(
        local,
        mesh=mesh,
        in_specs=(
            P("member", "lat", None, None),
            P(),
            P("lat", None, None),
            P(),
            P(),
            P(),
            P(None, "lat", None),
        ),
        out_specs=P("member", None, "lat", None),
        check_vma=False,
    )
```

profile of v0, /device:TPU:0, one launch (start us, length us, event | category | flops | bytes accessed | tf_op | source)
XLA Modules:
  0.0 60.7 jit_solution(4302945816617241693)
XLA Ops:
  0.0 1.6 %slice_bitcast_fusion.1 = (bf16[4,720,128]{2,1,0:T(8,128)(2,1)S(1)}, bf16[4,720,128]{2,1,0:T(8,128)(2,1)S(1)}) fusion(bf16[1,8,720,128]{3,2,1,0:T(8,128)(2,1)} %param.8), kind=kLoop, calls=%fused_computation.16 | loop fusion | bytes 2949120 | tf_op jit(solution)/shard_map/slice | solution.py:17
  1.6 3.3 %collective-permute-start = (bf16[4,720,128]{2,1,0:T(8,128)(2,1)S(1)}, bf16[4,720,128]{2,1,0:T(8,128)(2,1)}, u32[]{:S(2)}, u32[]{:S(2)}) collective-permute-start(bf16[4,720,128]{2,1,0:T(8,128)(2,1)S(1)} %get-tuple-element.9), channel_id=1, source_target_pairs={{0,1},{1,2},{2,3},{3,4},{4,5},{5,6},{6,7},{8,9},{9,10},{10,11},{11... | collective-permute-start | bytes 2211848 | tf_op jit(solution)/shard_map/ppermute | solution.py:16
  4.9 1.3 %collective-permute-start.1 = (bf16[4,720,128]{2,1,0:T(8,128)(2,1)S(1)}, bf16[4,720,128]{2,1,0:T(8,128)(2,1)}, u32[]{:S(2)}, u32[]{:S(2)}) collective-permute-start(bf16[4,720,128]{2,1,0:T(8,128)(2,1)S(1)} %get-tuple-element.10), channel_id=1, source_target_pairs={{1,0},{2,1},{3,2},{4,3},{5,4},{6,5},{7,6},{9,8},{10,9},{11,10},{12... | collective-permute-start | bytes 2211848 | tf_op jit(solution)/shard_map/ppermute | solution.py:19
  6.2 4.2 %collective-permute-done.1 = bf16[4,720,128]{2,1,0:T(8,128)(2,1)} collective-permute-done((bf16[4,720,128]{2,1,0:T(8,128)(2,1)S(1)}, bf16[4,720,128]{2,1,0:T(8,128)(2,1)}, u32[]{:S(2)}, u32[]{:S(2)}) %collective-permute-start.1) | collective-permute-done | bytes 737312 | tf_op jit(solution)/shard_map/ppermute | solution.py:19
  10.4 5.2 %add_convert_fusion = bf16[8,720,128]{2,1,0:T(8,128)(2,1)S(1)} fusion(bf16[8,720,128]{2,1,0:T(8,128)(2,1)S(1)} %bitcast.66, bf16[9,128,128]{2,1,0:T(8,128)(2,1)S(1)} %copy-done, bf16[4,720,128]{2,1,0:T(8,128)(2,1)} %collective-permute-done.1, bf16[4,720,128]{2,1,0:T(8,128)(2,1)} %collective-permute-done), kind=kOutput, calls=%fused_computation.6 | convolution fusion | flops 1706803200 | bytes 4718592 | tf_op jit(solution)/shard_map/conv_general_dilated | solution.py:123
  15.7 0.7 %fusion.26 = f32[32,8,720]{2,0,1:T(8,128)S(1)} fusion(bf16[8,720,128]{2,1,0:T(8,128)(2,1)S(1)} %add_convert_fusion, bf16[128,16]{0,1:T(8,128)(2,1)S(1)} %get-tuple-element.16, bf16[128,16]{0,1:T(8,128)(2,1)S(1)} %get-tuple-element.15), kind=kOutput, calls=%fused_computation.45 | convolution fusion | flops 47202304 | bytes 2220032 | tf_op jit(solution)/shard_map/anc,cg->gan/dot_general | solution.py:141
  16.4 0.7 %copy.53 = bf16[16,8,720]{2,1,0:T(8,128)(2,1)} copy(bf16[16,8,720]{2,0,1:T(8,128)(2,1)S(1)} %fusion.12) | data formatting | bytes 368640 | tf_op jit(solution)/shard_map/convert_element_type | solution.py:142
  17.1 1.1 %convolution_convert_fusion.1 = bf16[8,128,128]{1,2,0:T(8,128)(2,1)} fusion(bf16[8,720,128]{2,1,0:T(8,128)(2,1)S(1)} %add_convert_fusion, bf16[720,128,1]{1,0,2:T(8,128)(2,1)S(1)} %copy-done.6), kind=kOutput, calls=%fused_computation.11 | convolution fusion | flops 188874752 | bytes 1921024 | tf_op jit(solution)/shard_map/nk,anc->akc/dot_general | solution.py:138
  18.3 24.3 %shard_map.82 = (bf16[8,8,16,128]{3,2,1,0:T(8,128)(2,1)}, bf16[4,128,720]{2,1,0:T(8,128)(2,1)}) custom-call(bf16[8,8,16,128]{3,2,1,0:T(8,128)(2,1)} %bitcast.69, bf16[128,720]{1,0:T(8,128)(2,1)} %bitcast.70), custom_call_target="tpu_custom_call" | custom-call | tf_op jit(solution)/shard_map/pallas_call | solution.py:104
  42.6 1.2 %fusion.18 = f32[8,64,2,128]{3,1,2,0:T(8,128)S(1)} fusion(bf16[64,2,8,128]{3,2,1,0:T(8,128)(2,1)} %bitcast.71, bf16[8,64,64]{2,1,0:T(8,128)(2,1)S(1)} %copy-done.3, f32[64]{0:T(128)S(1)} %copy-done.9), kind=kOutput, calls=%fused_computation.29 | convolution fusion | flops 16875520 | bytes 852224 | tf_op jit(solution)/shard_map/mla,armc->mlrc/dot_general | solution.py:153
  43.8 0.1 subtract_convert_fusion
  43.9 0.3 fusion.7
  44.1 0.3 fusion.16
  44.4 0.2 fusion.11
  44.6 0.1 copy.52
  44.7 0.8 %reshape.28.narrow = bf16[8,16,128]{2,1,0:T(8,128)(2,1)} reshape(bf16[8,16,8,16]{3,2,1,0:T(8,128)(2,1)S(1)} %bitcast.68) | data formatting | bytes 65536 | tf_op jit(solution)/shard_map/reshape | solution.py:170
  45.5 10.0 %shard_map.83 = bf16[32,16,128]{2,1,0:T(8,128)(2,1)} custom-call(bf16[8,16,128]{2,1,0:T(8,128)(2,1)} %reshape.28.narrow), custom_call_target="tpu_custom_call" | custom-call | tf_op jit(solution)/shard_map/pallas_call | solution.py:104
  55.5 1.8 %reshape.29 = bf16[4,128,8,16]{3,2,1,0:T(8,128)(2,1)S(1)} reshape(bf16[32,16,128]{2,1,0:T(8,128)(2,1)} %shard_map.83) | data formatting | bytes 262144 | tf_op jit(solution)/shard_map/reshape | solution.py:174
  57.3 0.1 bitcast_convert_fusion
  57.5 1.2 %fusion.6 = f32[4,16,8,720]{3,1,2,0:T(8,128)S(1)} fusion(f32[4,16,8,720]{3,2,1,0:T(8,128)S(1)} %bitcast_convert_fusion, bf16[720,128,1,1]{1,0,3,2:T(8,128)(2,1)S(1)} %copy-done.5, bf16[4,128,8,16]{3,2,1,0:T(8,128)(2,1)S(1)} %reshape.29), kind=kOutput, calls=%fused_computation.8 | convolution fusion | flops 95109120 | bytes 3264512 | tf_op jit(solution)/shard_map/jkaf,nk->jfan/dot_general | solution.py:172
  58.7 0.3 multiply_reduce_fusion
  59.1 0.5 copy-done.4
  59.6 0.1 subtract_bitcast_fusion
  59.7 1.0 %copy.33 = f32[1,16,8,720]{3,2,1,0:T(8,128)} copy(f32[1,16,8,720]{3,1,2,0:T(8,128)S(1)} %subtract_bitcast_fusion) | data formatting | bytes 737280 | tf_op jit(solution)/shard_map/broadcast_in_dim | solution.py:183
  (24 shorter events, 0.1 us)
Async XLA Ops:
  0.0 10.4 %copy-start = (bf16[9,128,128]{2,1,0:T(8,128)(2,1)S(1)}, bf16[9,128,128]{2,1,0:T(8,128)(2,1)}, u32[]{:S(2)}) copy-start(bf16[9,128,128]{2,1,0:T(8,128)(2,1)} %param.9) | copy-start | bytes 884740
  0.0 10.4 %copy-start.1 = (bf16[1,8,720,128]{3,2,1,0:T(8,128)(2,1)S(1)}, bf16[1,8,720,128]{3,2,1,0:T(8,128)(2,1)}, u32[]{:S(2)}) copy-start(bf16[1,8,720,128]{3,2,1,0:T(8,128)(2,1)} %param.8) | copy-start | bytes 4423684
  0.0 6.2 %copy-start.8 = (f32[128,16]{0,1:T(8,128)S(1)}, f32[128,16]{0,1:T(8,128)}, u32[]{:S(2)}) copy-start(f32[128,16]{0,1:T(8,128)} %param.13) | copy-start | bytes 24580
  0.0 6.2 %copy-start.7 = (f32[2,64,128]{2,1,0:T(8,128)S(1)}, f32[2,64,128]{2,1,0:T(8,128)}, u32[]{:S(2)}) copy-start(f32[2,64,128]{2,1,0:T(8,128)} %param.12) | copy-start | bytes 196612
  1.6 4.6 %collective-permute-start = (bf16[4,720,128]{2,1,0:T(8,128)(2,1)S(1)}, bf16[4,720,128]{2,1,0:T(8,128)(2,1)}, u32[]{:S(2)}, u32[]{:S(2)}) collective-permute-start(bf16[4,720,128]{2,1,0:T(8,128)(2,1)S(1)} %get-tuple-element.9), channel_id=1, source_target_pairs={{0,1},{1,2},{2,3},{3,4},{4,5},{5,6},{6,7},{8,9},{9,10},{10,11},{11... | collective-permute-start | bytes 2211848 | tf_op jit(solution)/shard_map/ppermute | solution.py:16
  4.9 5.5 %collective-permute-start.1 = (bf16[4,720,128]{2,1,0:T(8,128)(2,1)S(1)}, bf16[4,720,128]{2,1,0:T(8,128)(2,1)}, u32[]{:S(2)}, u32[]{:S(2)}) collective-permute-start(bf16[4,720,128]{2,1,0:T(8,128)(2,1)S(1)} %get-tuple-element.10), channel_id=1, source_target_pairs={{1,0},{2,1},{3,2},{4,3},{5,4},{6,5},{7,6},{9,8},{10,9},{11,10},{12... | collective-permute-start | bytes 2211848 | tf_op jit(solution)/shard_map/ppermute | solution.py:19
  15.7 1.5 %copy-start.6 = (bf16[720,128,1]{1,0,2:T(8,128)(2,1)S(1)}, bf16[720,128,1]{1,0,2:T(8,128)(2,1)}, u32[]{:S(2)}) copy-start(bf16[720,128,1]{1,0,2:T(8,128)(2,1)} %constant.26) | copy-start | bytes 552964
  16.4 26.2 %copy-start.3 = (bf16[8,64,64]{2,1,0:T(8,128)(2,1)S(1)}, bf16[8,64,64]{2,1,0:T(8,128)(2,1)}, u32[]{:S(2)}) copy-start(bf16[8,64,64]{2,1,0:T(8,128)(2,1)} %param.10) | copy-start | bytes 196612
  16.4 26.2 %copy-start.9 = (f32[64]{0:T(128)S(1)}, f32[64]{0:T(128)}, u32[]{:S(2)}) copy-start(f32[64]{0:T(128)} %param.11) | copy-start | bytes 772
  44.4 12.9 %copy-start.2 = (bf16[4,128,720]{2,1,0:T(8,128)(2,1)S(1)}, bf16[4,128,720]{2,1,0:T(8,128)(2,1)}, u32[]{:S(2)}) copy-start(bf16[4,128,720]{2,1,0:T(8,128)(2,1)} %get-tuple-element.7) | copy-start | bytes 2211844
  55.5 2.0 %copy-start.5 = (bf16[720,128,1,1]{1,0,3,2:T(8,128)(2,1)S(1)}, bf16[720,128,1,1]{1,0,3,2:T(8,128)(2,1)}, u32[]{:S(2)}) copy-start(bf16[720,128,1,1]{1,0,3,2:T(8,128)(2,1)} %constant.27) | copy-start | bytes 552964
  58.7 0.9 %copy-start.4 = (bf16[16,8,720]{2,1,0:T(8,128)(2,1)S(1)}, bf16[16,8,720]{2,1,0:T(8,128)(2,1)}, u32[]{:S(2)}) copy-start(bf16[16,8,720]{2,1,0:T(8,128)(2,1)} %param.14) | copy-start | bytes 552964
where the time goes:
time: 61.1 us; the launch traced here: 60.7 us
  Pallas kernels  34.3 us (56%)
  matrix products  9.92 us (16%)
  local copies, waits for them, and re-layouts  6.59 us (11%)
  starting transfers between devices  4.57 us (7%)
  waiting for transfers between devices  4.19 us (7%)
  other arithmetic  0.9 us (1%)
    pallas_call x2, Pallas kernels, exchange(): pl.pallas_call(kernel, out_shape=[jax.ShapeDtypeStruct(shape, jnp.bfloat1...  34.3 us
    conv_general_dilated x1, matrix products, local(): lax.conv_general_dilated(padded, conv_weight, window_strides=(1,), paddin...  5.22 us
    ppermute x1, waiting for transfers between devices, with_halo(): lax.ppermute(lax.slice_in_dim(block, 0, width, axis=dim), axis, backward)  4.19 us
    ppermute x1, starting transfers between devices, with_halo(): lax.ppermute(lax.slice_in_dim(block, block.shape[dim] - width, None, axis...  3.29 us
    reshape x1, local copies, waits for them, and re-layouts, local(): spectra.reshape(members, 2 * modes, lat_rows, fields)  1.79 us
    slice x1, local copies, waits for them, and re-layouts, with_halo(): lax.slice_in_dim(block, block.shape[dim] - width, None, axis=dim)  1.57 us
    ppermute x1, starting transfers between devices, with_halo(): lax.ppermute(lax.slice_in_dim(block, 0, width, axis=dim), axis, backward)  1.28 us
  transfers between devices with their start and end apart: 2, of which 1 were waited for; matrix products, arithmetic and copies ran while one was open for 0% of the time, Pallas kernels for 0%

commit v1 on v0

v1 whole, which is shorter than its diff:
```python
import functools
import jax
import jax.numpy as jnp
import numpy as np
from jax import lax
from jax.experimental import pallas as pl
from jax.experimental.pallas import tpu as pltpu
from jax.sharding import PartitionSpec as P

MESH = pl.DeviceIdType.MESH
HALF = 4
F32 = jnp.float32
BF16 = jnp.bfloat16


def dft_table(nlon, modes, bands):
    phase = np.arange(nlon)[:, None] * np.arange(modes)[None, :] % nlon
    angle = phase * (2.0 * np.pi / nlon)
    table = np.stack([np.cos(angle), -np.sin(angle)], axis=1) / np.sqrt(nlon)
    table = table.reshape(nlon, 2, bands, modes // bands).swapaxes(1, 2)
    return jnp.asarray(table.reshape(nlon, 2 * modes).T.astype(np.float32), BF16)


def dot(a, b, contract=((1,), (0,))):
    return lax.dot_general(a, b, (contract, ((), ())), preferred_element_type=F32)


def smooth(diff):
    return diff * lax.rsqrt(diff * diff + 0.25)


def pick(shape, axis, cond):
    return jnp.where(cond(lax.broadcasted_iota(jnp.int32, shape, axis)), 1.0, 0.0)


def kernel(
    members,
    bands,
    state,
    conv_hbm,
    leg_hbm,
    quad_hbm,
    gain_hbm,
    proj_hbm,
    target_hbm,
    table_hbm,
    out_hbm,
    rows,
    conv_w,
    leg,
    quad,
    gain,
    proj,
    target,
    table,
    toeplitz,
    mixed,
    spec,
    banded,
    spread,
    wtable,
    legx,
    filt,
    filtw,
    wrep,
    drep,
    directs,
    narrowf,
    narrow,
    everyone,
    grads,
    load_sems,
    halo_sems,
    send_sems,
    spec_sems,
    direct_sems,
    back_sem,
    out_sem,
    lat_sems,
    member_sems,
):
    member, band = lax.axis_index("member"), lax.axis_index("lat")
    _, lat_rows, nlon, chans = state.shape
    pairs = lat_rows // 2
    nlat = bands * lat_rows
    mb, degrees = leg.shape[0], leg.shape[1]
    wide = 2 * mb
    fields = proj.shape[0]
    fa = fields * lat_rows
    has_low, has_high = band > 0, band < bands - 1

    barrier = pltpu.get_barrier_semaphore()
    hops = [1 << i for i in range((members - 1).bit_length())]

    def greet_lat(sem, dist):
        @pl.when(band >= dist)
        def _():
            pl.semaphore_signal(sem, 1, device_id=(member, band - dist), device_id_type=MESH)

        @pl.when(band + dist < bands)
        def _():
            pl.semaphore_signal(sem, 1, device_id=(member, band + dist), device_id_type=MESH)

    def count_lat(dist):
        return (band >= dist).astype(jnp.int32) + (band + dist < bands).astype(jnp.int32)

    greet_lat(barrier, 1)
    for hop in hops:
        pl.semaphore_signal(barrier, 1, device_id=(member ^ hop, band), device_id_type=MESH)
    loads = [
        (state.at[0], rows.at[pl.ds(HALF, lat_rows)]),
        (conv_hbm, conv_w),
        (table_hbm, table),
        (leg_hbm, leg),
        (quad_hbm, quad),
        (gain_hbm, gain),
        (proj_hbm, proj),
        (target_hbm, target),
    ]
    loads = [pltpu.make_async_copy(a, b, load_sems.at[i]) for i, (a, b) in enumerate(loads)]
    for copy in loads:
        copy.start()
    pl.semaphore_wait(barrier, count_lat(1) + len(hops))

    rounds = []
    known = 1
    while known < bands - 1:
        rounds.append(known)
        known *= 2

    def round_signal(i):
        if i < len(rounds):
            greet_lat(lat_sems.at[i], rounds[i])
        elif i < len(rounds) + len(hops):
            j = i - len(rounds)
            pl.semaphore_signal(
                member_sems.at[j], 1, device_id=(member ^ hops[j], band), device_id_type=MESH
            )

    def round_wait(i):
        if i < len(rounds):
            pl.semaphore_wait(lat_sems.at[i], count_lat(rounds[i]))
        elif i < len(rounds) + len(hops):
            pl.semaphore_wait(member_sems.at[i - len(rounds)], 1)

    def step_round(i):
        round_wait(i)
        round_signal(i + 1)

    round_signal(0)

    def halo(up, far):
        if up:
            src = lat_rows - 2 - 2 * far
            dst = HALF - 2 - 2 * far
            peer = band + 1
        else:
            src = 2 * far
            dst = HALF + lat_rows + 2 * far
            peer = band - 1
        sem = 2 * (0 if up else 1) + far
        return pltpu.make_async_remote_copy(
            state.at[0, pl.ds(src, 2)],
            rows.at[pl.ds(dst, 2)],
            send_sems.at[sem],
            halo_sems.at[sem],
            device_id=(member, peer),
            device_id_type=MESH,
        )

    for far in (0, 1):

        @pl.when(has_high)
        def _():
            halo(True, far).start()

        @pl.when(has_low)
        def _():
            halo(False, far).start()

    @pl.when(jnp.logical_not(has_low))
    def _():
        rows[0:HALF] = jnp.zeros((HALF, nlon, chans), BF16)

    @pl.when(jnp.logical_not(has_high))
    def _():
        rows[HALF + lat_rows :] = jnp.zeros((HALF, nlon, chans), BF16)

    def halo_wait(low, far):
        @pl.when(has_low if low else has_high)
        def _():
            halo(low, far).wait_recv()

    loads[1].wait()
    taps = conv_w.shape[0]
    for d in range(HALF + 1):
        for e in (0, 1):
            for f in (0, 1):
                tap = 2 * d + e - f
                w = conv_w[tap] if 0 <= tap < taps else jnp.zeros((chans, chans), BF16)
                at = (2 * d + e) * chans
                toeplitz[at : at + chans, f * chans : (f + 1) * chans] = w
    step_round(0)

    even = band % 2 == 0

    def pair_of(t):
        return jnp.where(even, pairs - 1 - t, t)

    def convolve(t):
        p = pair_of(t)
        window = [rows[2 * p + j] for j in range(2 * HALF + 2)]
        conv = dot(jnp.concatenate(window, axis=1), toeplitz[...])
        own = jnp.concatenate([rows[2 * p + HALF], rows[2 * p + HALF + 1]], axis=1)
        half = conv * 0.5
        mixed[p] = (own.astype(F32) + half + half * jnp.tanh(half)).astype(BF16)

    def transform(t):
        p = pair_of(t)
        s = dot(table[...], mixed[p]).astype(BF16)
        for e in (0, 1):
            spec[p, :, e] = s[:, e * chans : (e + 1) * chans].reshape(bands, wide, chans)

    def send_spec(t):
        p = pair_of(t)

        @pl.loop(1, bands)
        def _(k):
            peer = (band + k) % bands
            pltpu.make_async_remote_copy(
                spec.at[p, peer], banded.at[band, p], send_sems.at[4], spec_sems.at[t],
                device_id=(member, peer), device_id_type=MESH,
            ).start()

        pltpu.make_async_copy(spec.at[p, band], banded.at[band, p], spec_sems.at[t]).start()

    loads[0].wait()

    @pl.when(even)
    def _():
        halo_wait(False, 0)
        halo_wait(False, 1)

    @pl.when(jnp.logical_not(even))
    def _():
        halo_wait(True, 0)
        halo_wait(True, 1)

    convolve(0)
    step_round(1)
    loads[2].wait()
    transform(0)
    convolve(1)
    step_round(2)
    transform(1)
    for i in range(3, len(rounds)):
        step_round(i)

    for copy in loads[3:]:
        copy.wait()
    wtable[...] = (leg[...].astype(F32) * quad[...]).astype(BF16)
    flat_leg = leg[...].reshape(mb * degrees, nlat)

    @pl.loop(0, bands)
    def _(s):
        at = lax.broadcasted_iota(jnp.int32, (nlat, fa), 0)
        lane = lax.broadcasted_iota(jnp.int32, (nlat, fa), 1)
        onehot = jnp.where(at == s * lat_rows + lane % lat_rows, 1.0, 0.0).astype(BF16)
        legx[s] = dot(flat_leg, onehot).astype(BF16)

    high = proj[...].astype(BF16)
    low = (proj[...] - high.astype(F32)).astype(BF16)
    r0 = lax.broadcasted_iota(jnp.int32, (fa, fields), 0)
    r1 = lax.broadcasted_iota(jnp.int32, (fa, fields), 1)
    repeat = jnp.where(r0 // lat_rows == r1, 1.0, 0.0).astype(BF16)
    arow = lax.broadcasted_iota(jnp.int32, (fa, chans), 0) % lat_rows
    for i, part in enumerate((high, low)):
        wide_rows = dot(repeat, part)
        wrep[i * chans : (i + 1) * chans, :] = wide_rows.T.astype(BF16)
        for a in range(lat_rows):
            drep[i * fa : (i + 1) * fa, a * chans : (a + 1) * chans] = jnp.where(
                arow == a, wide_rows, 0.0
            ).astype(BF16)

    @pl.when(even)
    def _():
        halo_wait(True, 0)

    @pl.when(jnp.logical_not(even))
    def _():
        halo_wait(False, 0)

    for t in range(2, pairs - 1):
        convolve(t)
        transform(t)
    for i in range(max(3, len(rounds)), len(rounds) + len(hops)):
        step_round(i)

    @pl.when(even)
    def _():
        halo_wait(True, 1)

    @pl.when(jnp.logical_not(even))
    def _():
        halo_wait(False, 1)

    for t in range(pairs - 1):
        send_spec(t)
    convolve(pairs - 1)
    transform(pairs - 1)
    send_spec(pairs - 1)

    fine = dot(
        drep[...], jnp.concatenate([mixed[p] for p in range(pairs)], axis=1), ((1,), (1,))
    )
    directs[member] = (fine[:fa] + fine[fa:]).astype(BF16)

    @pl.loop(1, members)
    def _(k):
        peer = (member + k) % members
        pltpu.make_async_remote_copy(
            directs.at[member], directs.at[member], send_sems.at[5], direct_sems.at[0],
            device_id=(peer, band), device_id_type=MESH,
        ).start()

    for t in range(pairs):
        pltpu.make_async_copy(banded.at[:, t], banded.at[:, t], spec_sems.at[t]).wait()
    spread[...] = banded[...].astype(F32).reshape(nlat * wide, chans)
    gain_re, gain_im = gain[0], gain[1]
    for m in range(mb):
        re = spread[pl.ds(m, nlat, stride=wide), :]
        im = spread[pl.ds(mb + m, nlat, stride=wide), :]
        coef = dot(wtable[m], jnp.concatenate([re, im], axis=1).astype(BF16))
        c0, c1 = coef[:, :chans], coef[:, chans:]
        for r, part in enumerate((c0 * gain_re - c1 * gain_im, c0 * gain_im + c1 * gain_re)):
            part = part.astype(BF16)
            filt[m, r] = jnp.concatenate([part, part], axis=1)
    filtw[...] = dot(filt[...].reshape(mb * 2 * degrees, 2 * chans), wrep[...]).reshape(
        mb, 2, degrees, fa
    )

    @pl.loop(0, bands)
    def _(s):
        for m in range(mb):
            lx = legx[s, m * degrees : (m + 1) * degrees, :].astype(F32)
            for r in (0, 1):
                at = r * mb + m
                narrowf[s, at : at + 1, :] = jnp.sum(lx * filtw[m, r], axis=0, keepdims=True)

    narrow[...] = narrowf[...].astype(BF16)

    count = members * bands
    me = member * bands + band

    @pl.loop(1, count)
    def _(k):
        peer = (me + k) % count
        pltpu.make_async_remote_copy(
            narrow.at[peer % bands], everyone.at[me], send_sems.at[6], back_sem.at[0],
            device_id=(peer // bands, peer % bands), device_id_type=MESH,
        ).start()

    pltpu.make_async_copy(narrow.at[band], everyone.at[me], back_sem.at[0]).start()
    sent = directs.at[pl.ds(0, members - 1)]
    pltpu.make_async_copy(sent, sent, direct_sems.at[0]).wait()
    pltpu.make_async_copy(everyone, everyone, back_sem.at[0]).wait()

    def projected(j):
        k = everyone[pl.ds(j * bands, bands)].reshape(bands * wide, fa)
        synth = dot(k, table[...], ((0,), (0,)))
        return (directs[j].astype(F32) + synth).astype(BF16).astype(F32)

    own = projected(member)
    observed = target[...].astype(F32).reshape(fa, nlon)
    grads[...] = smooth(own - observed)

    @pl.loop(1, members)
    def _(k):
        grads[...] -= smooth(own - projected((member + k) % members)) * (1.0 / (members - 1))

    done = pltpu.make_async_copy(grads, out_hbm, out_sem.at[0])
    done.start()

    for far in (0, 1):

        @pl.when(has_high)
        def _():
            halo(True, far).wait_send()

        @pl.when(has_low)
        def _():
            halo(False, far).wait_send()

    sent = banded.at[pl.ds(0, bands - 1)]
    pltpu.make_async_copy(sent, sent, send_sems.at[4]).wait()
    sent = directs.at[pl.ds(0, members - 1)]
    pltpu.make_async_copy(sent, sent, send_sems.at[5]).wait()

    sent = everyone.at[pl.ds(0, count - 1)]
    pltpu.make_async_copy(sent, sent, send_sems.at[6]).wait()

    done.wait()


def local(state, conv_weight, legendre, quad_weight, spectral_gain, project_weight, target):
    _, lat_rows, nlon, chans = state.shape
    mb, degrees, nlat = legendre.shape
    members, bands = lax.axis_size("member"), lax.axis_size("lat")
    fields = project_weight.shape[1]
    fa, wide, pairs = fields * lat_rows, 2 * mb, lat_rows // 2
    table = dft_table(nlon, mb * bands, bands)
    vmem = pltpu.VMEM
    dma, plain = pltpu.SemaphoreType.DMA, pltpu.SemaphoreType.REGULAR
    out = pl.pallas_call(
        functools.partial(kernel, members, bands),
        out_shape=jax.ShapeDtypeStruct((fa, nlon), F32),
        in_specs=[pl.BlockSpec(memory_space=pl.ANY)] * 8,
        out_specs=pl.BlockSpec(memory_space=pl.ANY),
        scratch_shapes=[
            vmem((lat_rows + 2 * HALF, nlon, chans), BF16),
            vmem(conv_weight.shape, BF16),
            vmem(legendre.shape, BF16),
            vmem((1, nlat), F32),
            vmem(spectral_gain.shape, F32),
            vmem((fields, chans), F32),
            vmem(target.shape, BF16),
            vmem(table.shape, BF16),
            vmem(((2 * HALF + 2) * chans, 2 * chans), BF16),
            vmem((pairs, nlon, 2 * chans), BF16),
            vmem((pairs, bands, 2, wide, chans), BF16),
            vmem((bands, pairs, 2, wide, chans), BF16),
            vmem((nlat * wide, chans), F32),
            vmem(legendre.shape, BF16),
            vmem((bands, mb * degrees, fa), BF16),
            vmem((mb, 2, degrees, 2 * chans), BF16),
            vmem((mb, 2, degrees, fa), F32),
            vmem((2 * chans, fa), BF16),
            vmem((2 * fa, lat_rows * chans), BF16),
            vmem((members, fa, nlon), BF16),
            vmem((bands, wide, fa), F32),
            vmem((bands, wide, fa), BF16),
            vmem((members * bands, wide, fa), BF16),
            vmem((fa, nlon), F32),
            dma((8,)),
            dma((4,)),
            dma((7,)),
            dma((pairs,)),
            dma((1,)),
            dma((1,)),
            dma((1,)),
            plain((max(1, (bands - 1).bit_length()),)),
            plain((max(1, (members - 1).bit_length()),)),
        ],
        compiler_params=pltpu.CompilerParams(
            collective_id=0, has_side_effects=True, vmem_limit_bytes=60 * 1024 * 1024
        ),
    )(
        state,
        conv_weight,
        legendre,
        quad_weight.reshape(1, nlat),
        spectral_gain,
        project_weight.T,
        target,
        table,
    )
    return out.reshape(1, fields, lat_rows, nlon)


def solution(mesh):
    return jax.shard_map(
        local,
        mesh=mesh,
        in_specs=(
            P("member", "lat", None, None),
            P(),
            P("lat", None, None),
            P(),
            P(),
            P(),
            P(None, "lat", None),
        ),
        out_specs=P("member", None, "lat", None),
        check_vma=False,
    )
```

time: 61.1 us -> 32.7 us (0.54)
  matrix products: 9.92 us -> 0 us
  local copies, waits for them, and re-layouts: 6.59 us -> 1.77 us
  starting transfers between devices: 4.57 us -> 0 us
  waiting for transfers between devices: 4.19 us -> 0 us
  Pallas kernels: 34.3 us -> 30.8 us
  other arithmetic: 0.9 us -> 0 us
    conv_general_dilated x1 -> x0, matrix products: 5.22 us -> none  [local(): lax.conv_general_dilated(padded, conv_weight, window_strides=(1,), paddin...]
    dot_general x6 -> x0, matrix products: 4.7 us -> none  [the longest x1 1.22 us: local(): jnp.einsum('jkaf,nk->jfan', spectra.reshape(members, 2 * modes, lat_rows,...]
    ppermute x2 -> x0, starting transfers between devices: 4.57 us -> none  [the longest x1 3.29 us: with_halo(): lax.ppermute(lax.slice_in_dim(block, block.shape[dim] - width, None, axis...]
    ppermute x2 -> x0, waiting for transfers between devices: 4.19 us -> none  [the longest x1 4.19 us: with_halo(): lax.ppermute(lax.slice_in_dim(block, 0, width, axis=dim), axis, backward)]
    pallas_call x2 -> x1, Pallas kernels: 34.3 us -> 30.8 us  [local(): pl.pallas_call(functools.partial(kernel, members, bands), out_shape=jax.S...]
    reshape x3 -> x0, local copies, waits for them, and re-layouts: 2.66 us -> none  [the longest x1 1.79 us: local(): spectra.reshape(members, 2 * modes, lat_rows, fields)]
    slice x1 -> x0, local copies, waits for them, and re-layouts: 1.57 us -> none  [with_halo(): lax.slice_in_dim(block, block.shape[dim] - width, None, axis=dim)]
    unnamed x20 -> x1, local copies, waits for them, and re-layouts: 0.6 us -> 1.77 us
  transfers between devices with their start and end apart: 2 -> 0, of which waited for: 1 -> 0; matrix products, arithmetic and copies ran while one was open for 0% -> 0% of each run, Pallas kernels for 0% -> 0%
where the time goes in v1:
time: 32.7 us; the launch traced here: 32.6 us
  Pallas kernels  30.8 us (94%)
  local copies, waits for them, and re-layouts  1.77 us (5%)
    pallas_call x1, Pallas kernels, local(): pl.pallas_call(functools.partial(kernel, members, bands), out_shape=jax.S...  30.8 us
    unnamed x1, local copies, waits for them, and re-layouts  1.77 us

profile of v1, /device:TPU:0, one launch (start us, length us, event | category | flops | bytes accessed | tf_op | source)
XLA Modules:
  0.0 32.6 jit_solution(13034698684773388161)
XLA Ops:
  0.0 30.8 %shard_map.82 = f32[128,720]{1,0:T(8,128)} custom-call(bf16[1,8,720,128]{3,2,1,0:T(8,128)(2,1)} %state.1, bf16[9,128,128]{2,1,0:T(8,128)(2,1)} %conv_hbm.1, bf16[8,64,64]{2,1,0:T(8,128)(2,1)} %leg_hbm.1, f32[1,64]{1,0:T(1,128)} %bitcast.5, f32[2,64,128]{2,1,0:T(8,128)} %gain_hbm.1, f32[16,128]{1,0:T(8,128)} %bitcast.4, bf16[16,8,720]{2,1,0:T(8,128)(2,1)} %target_hbm.1, ...), custom_call_target="tpu_custom_call" | custom-call | tf_op jit(solution)/shard_map/pallas_call | solution.py:414
  30.8 1.8 %copy.10 = f32[1,16,8,720]{3,2,1,0:T(8,128)} copy(f32[1,16,8,720]{3,2,1,0:T(8,128)} %bitcast.3) | data formatting | bytes 737280

commit v2 on v1

--- a/solution.py
+++ b/solution.py
@@ -9,6 +9,7 @@
 
 MESH = pl.DeviceIdType.MESH
 HALF = 4
+LANES = 128
 F32 = jnp.float32
 BF16 = jnp.bfloat16
 
@@ -27,10 +28,6 @@
 
 def smooth(diff):
     return diff * lax.rsqrt(diff * diff + 0.25)
-
-
-def pick(shape, axis, cond):
-    return jnp.where(cond(lax.broadcasted_iota(jnp.int32, shape, axis)), 1.0, 0.0)
 
 
 def kernel(
@@ -44,7 +41,7 @@
     proj_hbm,
     target_hbm,
     table_hbm,
-    out_hbm,
+    out,
     rows,
     conv_w,
     leg,
@@ -68,14 +65,15 @@
     narrowf,
     narrow,
     everyone,
-    grads,
+    observed,
+    own_rows,
+    mine,
     load_sems,
     halo_sems,
     send_sems,
     spec_sems,
     direct_sems,
-    back_sem,
-    out_sem,
+    back_sems,
     lat_sems,
     member_sems,
 ):
@@ -87,6 +85,7 @@
     wide = 2 * mb
     fields = proj.shape[0]
     fa = fields * lat_rows
+    lanes = [slice(i, min(i + LANES, nlon)) for i in range(0, nlon, LANES)]
     has_low, has_high = band > 0, band < bands - 1
 
     barrier = pltpu.get_barrier_semaphore()
@@ -123,29 +122,26 @@
     pl.semaphore_wait(barrier, count_lat(1) + len(hops))
 
     rounds = []
+    for i, hop in enumerate(hops[1:]):
+        rounds.append((member_sems.at[i], hop, None))
     known = 1
     while known < bands - 1:
-        rounds.append(known)
+        rounds.append((lat_sems.at[len(rounds) - len(hops) + 1], None, known))
         known *= 2
 
     def round_signal(i):
         if i < len(rounds):
-            greet_lat(lat_sems.at[i], rounds[i])
-        elif i < len(rounds) + len(hops):
-            j = i - len(rounds)
-            pl.semaphore_signal(
-                member_sems.at[j], 1, device_id=(member ^ hops[j], band), device_id_type=MESH
-            )
-
-    def round_wait(i):
+            sem, hop, dist = rounds[i]
+            if hop is None:
+                greet_lat(sem, dist)
+            else:
+                pl.semaphore_signal(sem, 1, device_id=(member ^ hop, band), device_id_type=MESH)
+
+    def step_round(i):
         if i < len(rounds):
-            pl.semaphore_wait(lat_sems.at[i], count_lat(rounds[i]))
-        elif i < len(rounds) + len(hops):
-            pl.semaphore_wait(member_sems.at[i - len(rounds)], 1)
-
-    def step_round(i):
-        round_wait(i)
-        round_signal(i + 1)
+            sem, hop, dist = rounds[i]
+            pl.semaphore_wait(sem, 1 if hop is not None else count_lat(dist))
+            round_signal(i + 1)
 
     round_signal(0)
 
@@ -168,15 +164,22 @@
             device_id_type=MESH,
         )
 
-    for far in (0, 1):
-
-        @pl.when(has_high)
-        def _():
-            halo(True, far).start()
-
-        @pl.when(has_low)
-        def _():
-            halo(False, far).start()
+    even = band % 2 == 0
+
+    @pl.when(even & has_low)
+    def _():
+        halo(False, 0).start()
+        halo(False, 1).start()
+
+    @pl.when(has_high)
+    def _():
+        halo(True, 0).start()
+        halo(True, 1).start()
+
+    @pl.when(jnp.logical_not(even) & has_low)
+    def _():
+        halo(False, 0).start()
+        halo(False, 1).start()
 
     @pl.when(jnp.logical_not(has_low))
     def _():
@@ -200,10 +203,6 @@
                 w = conv_w[tap] if 0 <= tap < taps else jnp.zeros((chans, chans), BF16)
                 at = (2 * d + e) * chans
                 toeplitz[at : at + chans, f * chans : (f + 1) * chans] = w
-    step_round(0)
-
-    even = band % 2 == 0
-
     def pair_of(t):
         return jnp.where(even, pairs - 1 - t, t)
 
@@ -224,15 +223,54 @@
     def send_spec(t):
         p = pair_of(t)
 
-        @pl.loop(1, bands)
-        def _(k):
-            peer = (band + k) % bands
+        def to(peer):
             pltpu.make_async_remote_copy(
                 spec.at[p, peer], banded.at[band, p], send_sems.at[4], spec_sems.at[t],
                 device_id=(member, peer), device_id_type=MESH,
             ).start()
 
+        @pl.loop(1, bands)
+        def _(k):
+            dist = bands - k
+
+            @pl.when(band + dist < bands)
+            def _():
+                to(band + dist)
+
+            @pl.when(band >= dist)
+            def _():
+                to(band - dist)
+
         pltpu.make_async_copy(spec.at[p, band], banded.at[band, p], spec_sems.at[t]).start()
+
+    def direct(t):
+        p = pair_of(t)
+        fine = dot(drep[...], mixed[p], ((1,), (1,)))
+        half = 2 * fields
+        at = pl.ds(p * half, half)
+        directs[member, at] = (fine[:half] + fine[half:]).astype(BF16)
+
+        @pl.loop(1, members)
+        def _(k):
+            part = directs.at[member, at]
+            pltpu.make_async_remote_copy(
+                part, part, send_sems.at[5], direct_sems.at[0],
+                device_id=((member + k) % members, band), device_id_type=MESH,
+            ).start()
+
+    loads[6].wait()
+    high = proj[...].astype(BF16)
+    low = (proj[...] - high.astype(F32)).astype(BF16)
+    r0 = lax.broadcasted_iota(jnp.int32, (fa, fields), 0) % fields
+    r1 = lax.broadcasted_iota(jnp.int32, (fa, fields), 1)
+    tile = jnp.where(r0 == r1, 1.0, 0.0).astype(BF16)
+    for i, part in enumerate((high, low)):
+        wrep[i * chans : (i + 1) * chans, :] = dot(tile, part).T.astype(BF16)
+        for e in (0, 1):
+            at = (2 * i + e) * fields
+            drep[at : at + fields, e * chans : (e + 1) * chans] = part
+            drep[at : at + fields, (1 - e) * chans : (2 - e) * chans] = jnp.zeros_like(part)
+    step_round(0)
 
     loads[0].wait()
 
@@ -250,14 +288,14 @@
     step_round(1)
     loads[2].wait()
     transform(0)
+    direct(0)
     convolve(1)
     step_round(2)
     transform(1)
-    for i in range(3, len(rounds)):
-        step_round(i)
-
-    for copy in loads[3:]:
-        copy.wait()
+    direct(1)
+
+    for i in (3, 4, 5, 7):
+        loads[i].wait()
     wtable[...] = (leg[...].astype(F32) * quad[...]).astype(BF16)
     flat_leg = leg[...].reshape(mb * degrees, nlat)
 
@@ -265,22 +303,11 @@
     def _(s):
         at = lax.broadcasted_iota(jnp.int32, (nlat, fa), 0)
         lane = lax.broadcasted_iota(jnp.int32, (nlat, fa), 1)
-        onehot = jnp.where(at == s * lat_rows + lane % lat_rows, 1.0, 0.0).astype(BF16)
+        onehot = jnp.where(at == s * lat_rows + lane // fields, 1.0, 0.0).astype(BF16)
         legx[s] = dot(flat_leg, onehot).astype(BF16)
 
-    high = proj[...].astype(BF16)
-    low = (proj[...] - high.astype(F32)).astype(BF16)
-    r0 = lax.broadcasted_iota(jnp.int32, (fa, fields), 0)
-    r1 = lax.broadcasted_iota(jnp.int32, (fa, fields), 1)
-    repeat = jnp.where(r0 // lat_rows == r1, 1.0, 0.0).astype(BF16)
-    arow = lax.broadcasted_iota(jnp.int32, (fa, chans), 0) % lat_rows
-    for i, part in enumerate((high, low)):
-        wide_rows = dot(repeat, part)
-        wrep[i * chans : (i + 1) * chans, :] = wide_rows.T.astype(BF16)
-        for a in range(lat_rows):
-            drep[i * fa : (i + 1) * fa, a * chans : (a + 1) * chans] = jnp.where(
-                arow == a, wide_rows, 0.0
-            ).astype(BF16)
+    for i in range(3, len(rounds)):
+        step_round(i)
 
     @pl.when(even)
     def _():
@@ -290,11 +317,13 @@
     def _():
         halo_wait(False, 0)
 
+    send_spec(0)
+    send_spec(1)
     for t in range(2, pairs - 1):
         convolve(t)
         transform(t)
-    for i in range(max(3, len(rounds)), len(rounds) + len(hops)):
-        step_round(i)
+        send_spec(t)
+        direct(t)
 
     @pl.when(even)
     def _():
@@ -304,24 +333,16 @@
     def _():
         halo_wait(False, 1)
 
-    for t in range(pairs - 1):
-        send_spec(t)
     convolve(pairs - 1)
     transform(pairs - 1)
     send_spec(pairs - 1)
-
-    fine = dot(
-        drep[...], jnp.concatenate([mixed[p] for p in range(pairs)], axis=1), ((1,), (1,))
-    )
-    directs[member] = (fine[:fa] + fine[fa:]).astype(BF16)
-
-    @pl.loop(1, members)
-    def _(k):
-        peer = (member + k) % members
-        pltpu.make_async_remote_copy(
-            directs.at[member], directs.at[member], send_sems.at[5], direct_sems.at[0],
-            device_id=(peer, band), device_id_type=MESH,
-        ).start()
+    direct(pairs - 1)
+    for i, at in enumerate(lanes):
+        width = at.stop - at.start
+        own_rows[i, :, :width] = target[:, :, at].astype(F32).reshape(fa, width)
+        for a in range(lat_rows):
+            rows_of = own_rows[i, pl.ds(a, fields, stride=lat_rows), :]
+            observed[a * fields : (a + 1) * fields, at] = rows_of[:, :width]
 
     for t in range(pairs):
         pltpu.make_async_copy(banded.at[:, t], banded.at[:, t], spec_sems.at[t]).wait()
@@ -339,47 +360,68 @@
         mb, 2, degrees, fa
     )
 
-    @pl.loop(0, bands)
-    def _(s):
+    def strip(s):
         for m in range(mb):
             lx = legx[s, m * degrees : (m + 1) * degrees, :].astype(F32)
             for r in (0, 1):
                 at = r * mb + m
                 narrowf[s, at : at + 1, :] = jnp.sum(lx * filtw[m, r], axis=0, keepdims=True)
-
-    narrow[...] = narrowf[...].astype(BF16)
-
-    count = members * bands
+        narrow[s] = narrowf[s].astype(BF16)
+
     me = member * bands + band
 
-    @pl.loop(1, count)
+    def back(k, s):
+        pltpu.make_async_remote_copy(
+            narrow.at[s], everyone.at[me], send_sems.at[6], back_sems.at[member],
+            device_id=((member + k) % members, s), device_id_type=MESH,
+        ).start()
+
+    @pl.loop(1, bands)
+    def _(i):
+        s = jnp.where(band < bands // 2, bands - i, i - 1)
+        s = jnp.where(jnp.where(band < bands // 2, s <= band, s >= band), jnp.where(band < bands // 2, s - 1, s + 1), s)
+        strip(s)
+
+        @pl.loop(0, members)
+        def _(k):
+            back(k, s)
+
+    strip(band)
+
+    @pl.loop(1, members)
     def _(k):
-        peer = (me + k) % count
-        pltpu.make_async_remote_copy(
-            narrow.at[peer % bands], everyone.at[me], send_sems.at[6], back_sem.at[0],
-            device_id=(peer // bands, peer % bands), device_id_type=MESH,
-        ).start()
-
-    pltpu.make_async_copy(narrow.at[band], everyone.at[me], back_sem.at[0]).start()
-    sent = directs.at[pl.ds(0, members - 1)]
-    pltpu.make_async_copy(sent, sent, direct_sems.at[0]).wait()
-    pltpu.make_async_copy(everyone, everyone, back_sem.at[0]).wait()
+        back(k, band)
+
+    pltpu.make_async_copy(narrow.at[band], everyone.at[me], back_sems.at[member]).start()
+
+    def back_wait(j):
+        arrived = everyone.at[pl.ds(j * bands, bands)]
+        pltpu.make_async_copy(arrived, arrived, back_sems.at[j]).wait()
 
     def projected(j):
         k = everyone[pl.ds(j * bands, bands)].reshape(bands * wide, fa)
         synth = dot(k, table[...], ((0,), (0,)))
         return (directs[j].astype(F32) + synth).astype(BF16).astype(F32)
 
+    back_wait(member)
     own = projected(member)
-    observed = target[...].astype(F32).reshape(fa, nlon)
-    grads[...] = smooth(own - observed)
+    observed[...] = smooth(own - observed[...])
+    mine[...] = own
+    sent = directs.at[pl.ds(0, members - 1)]
+    pltpu.make_async_copy(sent, sent, direct_sems.at[0]).wait()
 
     @pl.loop(1, members)
     def _(k):
-        grads[...] -= smooth(own - projected((member + k) % members)) * (1.0 / (members - 1))
-
-    done = pltpu.make_async_copy(grads, out_hbm, out_sem.at[0])
-    done.start()
+        j = (member + k) % members
+        back_wait(j)
+        observed[...] -= smooth(mine[...] - projected(j)) * (1.0 / (members - 1))
+
+    for i, at in enumerate(lanes):
+        width = at.stop - at.start
+        own_rows[i, :, :width] = observed[:, at]
+        for f in range(fields):
+            rows_of = own_rows[i, pl.ds(f, lat_rows, stride=fields), :]
+            out[f * lat_rows : (f + 1) * lat_rows, at] = rows_of[:, :width]
 
     for far in (0, 1):
 
@@ -396,10 +438,8 @@
     sent = directs.at[pl.ds(0, members - 1)]
     pltpu.make_async_copy(sent, sent, send_sems.at[5]).wait()
 
-    sent = everyone.at[pl.ds(0, count - 1)]
+    sent = everyone.at[pl.ds(0, members * bands - 1)]
     pltpu.make_async_copy(sent, sent, send_sems.at[6]).wait()
-
-    done.wait()
 
 
 def local(state, conv_weight, legendre, quad_weight, spectral_gain, project_weight, target):
@@ -413,9 +453,9 @@
     dma, plain = pltpu.SemaphoreType.DMA, pltpu.SemaphoreType.REGULAR
     out = pl.pallas_call(
         functools.partial(kernel, members, bands),
-        out_shape=jax.ShapeDtypeStruct((fa, nlon), F32),
+        out_shape=pltpu.VMEM((fa, nlon), F32),
         in_specs=[pl.BlockSpec(memory_space=pl.ANY)] * 8,
-        out_specs=pl.BlockSpec(memory_space=pl.ANY),
+        out_specs=pl.BlockSpec(memory_space=pltpu.VMEM),
         scratch_shapes=[
             vmem((lat_rows + 2 * HALF, nlon, chans), BF16),
             vmem(conv_weight.shape, BF16),
@@ -435,19 +475,20 @@
             vmem((mb, 2, degrees, 2 * chans), BF16),
             vmem((mb, 2, degrees, fa), F32),
             vmem((2 * chans, fa), BF16),
-            vmem((2 * fa, lat_rows * chans), BF16),
+            vmem((4 * fields, 2 * chans), BF16),
             vmem((members, fa, nlon), BF16),
             vmem((bands, wide, fa), F32),
             vmem((bands, wide, fa), BF16),
             vmem((members * bands, wide, fa), BF16),
+            vmem((fa, nlon), F32),
+            vmem((pl.cdiv(nlon, LANES), fa, LANES), F32),
             vmem((fa, nlon), F32),
             dma((8,)),
             dma((4,)),
             dma((7,)),
             dma((pairs,)),
             dma((1,)),
-            dma((1,)),
-            dma((1,)),
+            dma((members,)),
             plain((max(1, (bands - 1).bit_length()),)),
             plain((max(1, (members - 1).bit_length()),)),
         ],

time: 32.7 us -> 29.1 us (0.89)
  Pallas kernels: 30.8 us -> 28.2 us
  local copies, waits for them, and re-layouts: 1.77 us -> 0.75 us
    pallas_call x1, Pallas kernels: 30.8 us -> 28.2 us  [local(): pl.pallas_call(functools.partial(kernel, members, bands), out_shape=pltpu...]
    unnamed x1, local copies, waits for them, and re-layouts: 1.77 us -> 0.75 us
where the time goes in v2:
time: 29.1 us; the launch traced here: 29 us
  Pallas kernels  28.2 us (97%)
  local copies, waits for them, and re-layouts  0.75 us (3%)
    pallas_call x1, Pallas kernels, local(): pl.pallas_call(functools.partial(kernel, members, bands), out_shape=pltpu...  28.2 us
    unnamed x1, local copies, waits for them, and re-layouts  0.75 us

profile of v2, /device:TPU:0, one launch (start us, length us, event | category | flops | bytes accessed | tf_op | source)
XLA Modules:
  0.0 29.0 jit_solution(8150352238973960575)
XLA Ops:
  0.0 28.2 %shard_map.82 = f32[128,720]{1,0:T(8,128)S(1)} custom-call(bf16[1,8,720,128]{3,2,1,0:T(8,128)(2,1)} %state.1, bf16[9,128,128]{2,1,0:T(8,128)(2,1)} %conv_hbm.1, bf16[8,64,64]{2,1,0:T(8,128)(2,1)} %leg_hbm.1, f32[1,64]{1,0:T(1,128)} %bitcast.5, f32[2,64,128]{2,1,0:T(8,128)} %gain_hbm.1, f32[16,128]{1,0:T(8,128)} %bitcast.4, bf16[16,8,720]{2,1,0:T(8,128)(2,1)} %target_hbm.1, ...), custom_call_target="tpu_custom_call" | custom-call | tf_op jit(solution)/shard_map/pallas_call | solution.py:454
  28.2 0.7 %copy.10 = f32[1,16,8,720]{3,2,1,0:T(8,128)} copy(f32[1,16,8,720]{3,2,1,0:T(8,128)S(1)} %bitcast.3) | data formatting | bytes 737280

commit v3 on v2

--- a/solution.py
+++ b/solution.py
@@ -56,13 +56,14 @@
     banded,
     spread,
     wtable,
-    legx,
+    leg_t,
+    gather,
+    masked,
     filt,
     filtw,
     wrep,
     drep,
     directs,
-    narrowf,
     narrow,
     everyone,
     observed,
@@ -76,6 +77,7 @@
     back_sems,
     lat_sems,
     member_sems,
+    left_sem,
 ):
     member, band = lax.axis_index("member"), lax.axis_index("lat")
     _, lat_rows, nlon, chans = state.shape
@@ -218,20 +220,19 @@
         p = pair_of(t)
         s = dot(table[...], mixed[p]).astype(BF16)
         for e in (0, 1):
-            spec[p, :, e] = s[:, e * chans : (e + 1) * chans].reshape(bands, wide, chans)
-
-    def send_spec(t):
-        p = pair_of(t)
+            spec[:, p, e] = s[:, e * chans : (e + 1) * chans].reshape(bands, wide, chans)
+
+    def send_spec(first, last):
+        at = pl.ds(jnp.where(even, pairs - 1 - last, first), last - first + 1)
+        arrival = spec_sems.at[first]
 
         def to(peer):
             pltpu.make_async_remote_copy(
-                spec.at[p, peer], banded.at[band, p], send_sems.at[4], spec_sems.at[t],
+                spec.at[peer, at], banded.at[band, at], send_sems.at[4], arrival,
                 device_id=(member, peer), device_id_type=MESH,
             ).start()
 
-        @pl.loop(1, bands)
-        def _(k):
-            dist = bands - k
+        for dist in range(bands - 1, 0, -1):
 
             @pl.when(band + dist < bands)
             def _():
@@ -241,7 +242,11 @@
             def _():
                 to(band - dist)
 
-        pltpu.make_async_copy(spec.at[p, band], banded.at[band, p], spec_sems.at[t]).start()
+        pltpu.make_async_copy(spec.at[band, at], banded.at[band, at], arrival).start()
+
+    def wait_spec(first, last):
+        part = banded.at[:, pl.ds(first, last - first + 1)]
+        pltpu.make_async_copy(part, part, spec_sems.at[first]).wait()
 
     def direct(t):
         p = pair_of(t)
@@ -255,7 +260,7 @@
             part = directs.at[member, at]
             pltpu.make_async_remote_copy(
                 part, part, send_sems.at[5], direct_sems.at[0],
-                device_id=((member + k) % members, band), device_id_type=MESH,
+                device_id=(member ^ k, band), device_id_type=MESH,
             ).start()
 
     loads[6].wait()
@@ -264,8 +269,11 @@
     r0 = lax.broadcasted_iota(jnp.int32, (fa, fields), 0) % fields
     r1 = lax.broadcasted_iota(jnp.int32, (fa, fields), 1)
     tile = jnp.where(r0 == r1, 1.0, 0.0).astype(BF16)
+    tiled = dot(tile, high).T.astype(BF16)
+    for r in (0, 1):
+        wrep[r * chans : (r + 1) * chans, r * fa : (r + 1) * fa] = tiled
+        wrep[r * chans : (r + 1) * chans, (1 - r) * fa : (2 - r) * fa] = jnp.zeros_like(tiled)
     for i, part in enumerate((high, low)):
-        wrep[i * chans : (i + 1) * chans, :] = dot(tile, part).T.astype(BF16)
         for e in (0, 1):
             at = (2 * i + e) * fields
             drep[at : at + fields, e * chans : (e + 1) * chans] = part
@@ -294,49 +302,27 @@
     transform(1)
     direct(1)
 
+    @pl.when(even)
+    def _():
+        halo_wait(True, 0)
+
+    @pl.when(jnp.logical_not(even))
+    def _():
+        halo_wait(False, 0)
+
+    for t in range(2, pairs - 1):
+        convolve(t)
+        transform(t)
+        direct(t)
+
     for i in (3, 4, 5, 7):
         loads[i].wait()
     wtable[...] = (leg[...].astype(F32) * quad[...]).astype(BF16)
-    flat_leg = leg[...].reshape(mb * degrees, nlat)
-
-    @pl.loop(0, bands)
-    def _(s):
-        at = lax.broadcasted_iota(jnp.int32, (nlat, fa), 0)
-        lane = lax.broadcasted_iota(jnp.int32, (nlat, fa), 1)
-        onehot = jnp.where(at == s * lat_rows + lane // fields, 1.0, 0.0).astype(BF16)
-        legx[s] = dot(flat_leg, onehot).astype(BF16)
-
-    for i in range(3, len(rounds)):
-        step_round(i)
-
-    @pl.when(even)
-    def _():
-        halo_wait(True, 0)
-
-    @pl.when(jnp.logical_not(even))
-    def _():
-        halo_wait(False, 0)
-
-    send_spec(0)
-    send_spec(1)
-    for t in range(2, pairs - 1):
-        convolve(t)
-        transform(t)
-        send_spec(t)
-        direct(t)
-
-    @pl.when(even)
-    def _():
-        halo_wait(True, 1)
-
-    @pl.when(jnp.logical_not(even))
-    def _():
-        halo_wait(False, 1)
-
-    convolve(pairs - 1)
-    transform(pairs - 1)
-    send_spec(pairs - 1)
-    direct(pairs - 1)
+    for m in range(mb):
+        leg_t[m] = leg[m].T
+    r0 = lax.broadcasted_iota(jnp.int32, (wide, wide * lat_rows), 0)
+    r1 = lax.broadcasted_iota(jnp.int32, (wide, wide * lat_rows), 1)
+    gather[...] = jnp.where(r1 // lat_rows == r0, 1.0, 0.0).astype(BF16)
     for i, at in enumerate(lanes):
         width = at.stop - at.start
         own_rows[i, :, :width] = target[:, :, at].astype(F32).reshape(fa, width)
@@ -344,8 +330,51 @@
             rows_of = own_rows[i, pl.ds(a, fields, stride=lat_rows), :]
             observed[a * fields : (a + 1) * fields, at] = rows_of[:, :width]
 
-    for t in range(pairs):
-        pltpu.make_async_copy(banded.at[:, t], banded.at[:, t], spec_sems.at[t]).wait()
+    for i in range(3, len(rounds)):
+        step_round(i)
+
+    send_spec(0, 0)
+
+    @pl.when(even & has_low)
+    def _():
+        halo(False, 0).wait_send()
+        halo(False, 1).wait_send()
+
+    @pl.when(jnp.logical_not(even) & has_high)
+    def _():
+        halo(True, 0).wait_send()
+        halo(True, 1).wait_send()
+
+    neighbour = band ^ 1
+    leaves = jnp.where(even, has_low, has_high)
+    near_leaves = jnp.where(even, neighbour < bands - 1, neighbour > 0)
+
+    @pl.when(leaves & jnp.logical_not(near_leaves))
+    def _():
+        pl.semaphore_signal(left_sem.at[0], 1, device_id=(member, neighbour), device_id_type=MESH)
+
+    @pl.when(near_leaves & jnp.logical_not(leaves))
+    def _():
+        pl.semaphore_wait(left_sem.at[0], 1)
+
+    send_spec(1, pairs - 2)
+
+    @pl.when(even)
+    def _():
+        halo_wait(True, 1)
+
+    @pl.when(jnp.logical_not(even))
+    def _():
+        halo_wait(False, 1)
+
+    convolve(pairs - 1)
+    transform(pairs - 1)
+    send_spec(pairs - 1, pairs - 1)
+    direct(pairs - 1)
+
+    wait_spec(0, 0)
+    wait_spec(1, pairs - 2)
+    wait_spec(pairs - 1, pairs - 1)
     spread[...] = banded[...].astype(F32).reshape(nlat * wide, chans)
     gain_re, gain_im = gain[0], gain[1]
     for m in range(mb):
@@ -353,45 +382,48 @@
         im = spread[pl.ds(mb + m, nlat, stride=wide), :]
         coef = dot(wtable[m], jnp.concatenate([re, im], axis=1).astype(BF16))
         c0, c1 = coef[:, :chans], coef[:, chans:]
-        for r, part in enumerate((c0 * gain_re - c1 * gain_im, c0 * gain_im + c1 * gain_re)):
-            part = part.astype(BF16)
-            filt[m, r] = jnp.concatenate([part, part], axis=1)
-    filtw[...] = dot(filt[...].reshape(mb * 2 * degrees, 2 * chans), wrep[...]).reshape(
-        mb, 2, degrees, fa
+        real, imag = c0 * gain_re - c1 * gain_im, c0 * gain_im + c1 * gain_re
+        filt[m] = jnp.concatenate([real, imag], axis=1).astype(BF16)
+    filtw[...] = (
+        dot(filt[...].reshape(mb * degrees, 2 * chans), wrep[...])
+        .astype(BF16)
+        .reshape(mb, degrees, 2 * fa)
     )
 
-    def strip(s):
-        for m in range(mb):
-            lx = legx[s, m * degrees : (m + 1) * degrees, :].astype(F32)
-            for r in (0, 1):
-                at = r * mb + m
-                narrowf[s, at : at + 1, :] = jnp.sum(lx * filtw[m, r], axis=0, keepdims=True)
-        narrow[s] = narrowf[s].astype(BF16)
+    r0 = lax.broadcasted_iota(jnp.int32, (nlat, fa), 0) % lat_rows
+    r1 = lax.broadcasted_iota(jnp.int32, (nlat, fa), 1) // fields
+    for m in range(mb):
+        synth = dot(leg_t[m], filtw[m])
+        for r in (0, 1):
+            kept = jnp.where(r0 == r1, synth[:, r * fa : (r + 1) * fa], 0.0).astype(BF16)
+            masked[:, r * mb + m] = kept.reshape(bands, lat_rows, fa)
+    for s in range(bands):
+        narrow[s] = dot(gather[...], masked[s].reshape(wide * lat_rows, fa)).astype(BF16)
 
     me = member * bands + band
 
     def back(k, s):
         pltpu.make_async_remote_copy(
             narrow.at[s], everyone.at[me], send_sems.at[6], back_sems.at[member],
-            device_id=((member + k) % members, s), device_id_type=MESH,
+            device_id=(member ^ k, s), device_id_type=MESH,
         ).start()
 
     @pl.loop(1, bands)
     def _(i):
-        s = jnp.where(band < bands // 2, bands - i, i - 1)
-        s = jnp.where(jnp.where(band < bands // 2, s <= band, s >= band), jnp.where(band < bands // 2, s - 1, s + 1), s)
-        strip(s)
-
-        @pl.loop(0, members)
-        def _(k):
-            back(k, s)
-
-    strip(band)
-
-    @pl.loop(1, members)
-    def _(k):
+        dist = bands - i
+
+        @pl.when(band + dist < bands)
+        def _():
+            for k in range(members):
+                back(members - 1 - k, band + dist)
+
+        @pl.when(band >= dist)
+        def _():
+            for k in range(members):
+                back(members - 1 - k, band - dist)
+
+    for k in range(1, members):
         back(k, band)
-
     pltpu.make_async_copy(narrow.at[band], everyone.at[me], back_sems.at[member]).start()
 
     def back_wait(j):
@@ -412,7 +444,7 @@
 
     @pl.loop(1, members)
     def _(k):
-        j = (member + k) % members
+        j = member ^ k
         back_wait(j)
         observed[...] -= smooth(mine[...] - projected(j)) * (1.0 / (members - 1))
 
@@ -423,15 +455,15 @@
             rows_of = own_rows[i, pl.ds(f, lat_rows, stride=fields), :]
             out[f * lat_rows : (f + 1) * lat_rows, at] = rows_of[:, :width]
 
-    for far in (0, 1):
-
-        @pl.when(has_high)
-        def _():
-            halo(True, far).wait_send()
-
-        @pl.when(has_low)
-        def _():
-            halo(False, far).wait_send()
+    @pl.when(even & has_high)
+    def _():
+        halo(True, 0).wait_send()
+        halo(True, 1).wait_send()
+
+    @pl.when(jnp.logical_not(even) & has_low)
+    def _():
+        halo(False, 0).wait_send()
+        halo(False, 1).wait_send()
 
     sent = banded.at[pl.ds(0, bands - 1)]
     pltpu.make_async_copy(sent, sent, send_sems.at[4]).wait()
@@ -467,17 +499,18 @@
             vmem(table.shape, BF16),
             vmem(((2 * HALF + 2) * chans, 2 * chans), BF16),
             vmem((pairs, nlon, 2 * chans), BF16),
-            vmem((pairs, bands, 2, wide, chans), BF16),
+            vmem((bands, pairs, 2, wide, chans), BF16),
             vmem((bands, pairs, 2, wide, chans), BF16),
             vmem((nlat * wide, chans), F32),
             vmem(legendre.shape, BF16),
-            vmem((bands, mb * degrees, fa), BF16),
-            vmem((mb, 2, degrees, 2 * chans), BF16),
-            vmem((mb, 2, degrees, fa), F32),
-            vmem((2 * chans, fa), BF16),
+            vmem((mb, nlat, degrees), BF16),
+            vmem((wide, wide * lat_rows), BF16),
+            vmem((bands, wide, lat_rows, fa), BF16),
+            vmem((mb, degrees, 2 * chans), BF16),
+            vmem((mb, degrees, 2 * fa), BF16),
+            vmem((2 * chans, 2 * fa), BF16),
             vmem((4 * fields, 2 * chans), BF16),
             vmem((members, fa, nlon), BF16),
-            vmem((bands, wide, fa), F32),
             vmem((bands, wide, fa), BF16),
             vmem((members * bands, wide, fa), BF16),
             vmem((fa, nlon), F32),
@@ -491,6 +524,7 @@
             dma((members,)),
             plain((max(1, (bands - 1).bit_length()),)),
             plain((max(1, (members - 1).bit_length()),)),
+            plain((1,)),
         ],
         compiler_params=pltpu.CompilerParams(
             collective_id=0, has_side_effects=True, vmem_limit_bytes=60 * 1024 * 1024

time: 29.1 us -> 28.1 us (0.966)
  Pallas kernels: 28.2 us -> 27.2 us
    pallas_call x1, Pallas kernels: 28.2 us -> 27.2 us  [local(): pl.pallas_call(functools.partial(kernel, members, bands), out_shape=pltpu...]
where the time goes in v3:
time: 28.1 us; the launch traced here: 28 us
  Pallas kernels  27.2 us (97%)
  local copies, waits for them, and re-layouts  0.75 us (3%)
    pallas_call x1, Pallas kernels, local(): pl.pallas_call(functools.partial(kernel, members, bands), out_shape=pltpu...  27.2 us
    unnamed x1, local copies, waits for them, and re-layouts  0.75 us

profile of v3, /device:TPU:0, one launch (start us, length us, event | category | flops | bytes accessed | tf_op | source)
XLA Modules:
  0.0 28.0 jit_solution(2576677079555368156)
XLA Ops:
  0.0 27.2 %shard_map.82 = f32[128,720]{1,0:T(8,128)S(1)} custom-call(bf16[1,8,720,128]{3,2,1,0:T(8,128)(2,1)} %state.1, bf16[9,128,128]{2,1,0:T(8,128)(2,1)} %conv_hbm.1, bf16[8,64,64]{2,1,0:T(8,128)(2,1)} %leg_hbm.1, f32[1,64]{1,0:T(1,128)} %bitcast.5, f32[2,64,128]{2,1,0:T(8,128)} %gain_hbm.1, f32[16,128]{1,0:T(8,128)} %bitcast.4, bf16[16,8,720]{2,1,0:T(8,128)(2,1)} %target_hbm.1, ...), custom_call_target="tpu_custom_call" | custom-call | tf_op jit(solution)/shard_map/pallas_call | solution.py:486
  27.2 0.7 %copy.10 = f32[1,16,8,720]{3,2,1,0:T(8,128)} copy(f32[1,16,8,720]{3,2,1,0:T(8,128)S(1)} %bitcast.3) | data formatting | bytes 737280

commit v4 on v3

--- a/solution.py
+++ b/solution.py
@@ -10,6 +10,7 @@
 MESH = pl.DeviceIdType.MESH
 HALF = 4
 LANES = 128
+VMEM_BYTES = 67043328
 F32 = jnp.float32
 BF16 = jnp.bfloat16
 
@@ -41,7 +42,11 @@
     proj_hbm,
     target_hbm,
     table_hbm,
-    out,
+    everyone,
+    directs,
+    table,
+    mine,
+    observed,
     rows,
     conv_w,
     leg,
@@ -49,7 +54,6 @@
     gain,
     proj,
     target,
-    table,
     toeplitz,
     mixed,
     spec,
@@ -63,12 +67,8 @@
     filtw,
     wrep,
     drep,
-    directs,
     narrow,
-    everyone,
-    observed,
     own_rows,
-    mine,
     load_sems,
     halo_sems,
     send_sems,
@@ -234,13 +234,15 @@
 
         for dist in range(bands - 1, 0, -1):
 
+            @pl.when(band >= dist)
+            def _():
+                to(band - dist)
+
+        for dist in range(bands - 1, 0, -1):
+
             @pl.when(band + dist < bands)
             def _():
                 to(band + dist)
-
-            @pl.when(band >= dist)
-            def _():
-                to(band - dist)
 
         pltpu.make_async_copy(spec.at[band, at], banded.at[band, at], arrival).start()
 
@@ -372,10 +374,18 @@
     send_spec(pairs - 1, pairs - 1)
     direct(pairs - 1)
 
+    def spread_rows(t):
+        for source in range(bands):
+            q = pairs - 1 - t if source % 2 == 0 else t
+            at = (source * pairs + q) * 2 * wide
+            spread[at : at + 2 * wide, :] = banded[source, q].astype(F32).reshape(2 * wide, chans)
+
     wait_spec(0, 0)
     wait_spec(1, pairs - 2)
+    for t in range(pairs - 1):
+        spread_rows(t)
     wait_spec(pairs - 1, pairs - 1)
-    spread[...] = banded[...].astype(F32).reshape(nlat * wide, chans)
+    spread_rows(pairs - 1)
     gain_re, gain_im = gain[0], gain[1]
     for m in range(mb):
         re = spread[pl.ds(m, nlat, stride=wide), :]
@@ -412,15 +422,19 @@
     def _(i):
         dist = bands - i
 
+        @pl.when(band >= dist)
+        def _():
+            for k in range(members):
+                back(members - 1 - k, band - dist)
+
+    @pl.loop(1, bands)
+    def _(i):
+        dist = bands - i
+
         @pl.when(band + dist < bands)
         def _():
             for k in range(members):
                 back(members - 1 - k, band + dist)
-
-        @pl.when(band >= dist)
-        def _():
-            for k in range(members):
-                back(members - 1 - k, band - dist)
 
     for k in range(1, members):
         back(k, band)
@@ -442,18 +456,13 @@
     sent = directs.at[pl.ds(0, members - 1)]
     pltpu.make_async_copy(sent, sent, direct_sems.at[0]).wait()
 
-    @pl.loop(1, members)
+    @pl.loop(1, members - 1)
     def _(k):
         j = member ^ k
         back_wait(j)
         observed[...] -= smooth(mine[...] - projected(j)) * (1.0 / (members - 1))
 
-    for i, at in enumerate(lanes):
-        width = at.stop - at.start
-        own_rows[i, :, :width] = observed[:, at]
-        for f in range(fields):
-            rows_of = own_rows[i, pl.ds(f, lat_rows, stride=fields), :]
-            out[f * lat_rows : (f + 1) * lat_rows, at] = rows_of[:, :width]
+    back_wait(member ^ (members - 1))
 
     @pl.when(even & has_high)
     def _():
@@ -472,6 +481,32 @@
 
     sent = everyone.at[pl.ds(0, members * bands - 1)]
     pltpu.make_async_copy(sent, sent, send_sems.at[6]).wait()
+
+
+def finish_kernel(
+    members, bands, everyone, directs, table, mine, grads, out, tiles, sorted_rows, sems
+):
+    fields, lat_rows, nlon = out.shape
+    last = lax.axis_index("member") ^ (members - 1)
+    fa = fields * lat_rows
+    k = everyone[pl.ds(last * bands, bands)].reshape(-1, fa).T
+    copies = []
+    for i, start in enumerate(range(0, nlon, LANES)):
+        width = min(LANES, nlon - start)
+        at = slice(start, start + width)
+        other = (directs[last, :, at].astype(F32) + dot(k, table[:, at])).astype(BF16)
+        term = smooth(mine[:, at] - other.astype(F32)) * (1.0 / (members - 1))
+        tiles[i, :, :width] = grads[:, at] - term
+        for f in range(fields):
+            rows_of = tiles[i, pl.ds(f, lat_rows, stride=fields), :]
+            sorted_rows[f, :, at] = rows_of[:, :width]
+        part = pl.ds(start, width)
+        copies.append(
+            pltpu.make_async_copy(sorted_rows.at[:, :, part], out.at[:, :, part], sems.at[i])
+        )
+        copies[-1].start()
+    for copy in copies:
+        copy.wait()
 
 
 def local(state, conv_weight, legendre, quad_weight, spectral_gain, project_weight, target):
@@ -483,11 +518,22 @@
     table = dft_table(nlon, mb * bands, bands)
     vmem = pltpu.VMEM
     dma, plain = pltpu.SemaphoreType.DMA, pltpu.SemaphoreType.REGULAR
-    out = pl.pallas_call(
+    results = [
+        vmem((members * bands, wide, fa), BF16),
+        vmem((members, fa, nlon), BF16),
+        vmem(table.shape, BF16),
+        vmem((fa, nlon), F32),
+        vmem((fa, nlon), F32),
+    ]
+    kept = sum(
+        int(np.prod(r.shape[:-1])) * pl.cdiv(r.shape[-1], LANES) * LANES * jnp.dtype(r.dtype).itemsize
+        for r in results
+    )
+    arrived = pl.pallas_call(
         functools.partial(kernel, members, bands),
-        out_shape=pltpu.VMEM((fa, nlon), F32),
+        out_shape=results,
         in_specs=[pl.BlockSpec(memory_space=pl.ANY)] * 8,
-        out_specs=pl.BlockSpec(memory_space=pltpu.VMEM),
+        out_specs=[pl.BlockSpec(memory_space=pltpu.VMEM)] * 5,
         scratch_shapes=[
             vmem((lat_rows + 2 * HALF, nlon, chans), BF16),
             vmem(conv_weight.shape, BF16),
@@ -496,7 +542,6 @@
             vmem(spectral_gain.shape, F32),
             vmem((fields, chans), F32),
             vmem(target.shape, BF16),
-            vmem(table.shape, BF16),
             vmem(((2 * HALF + 2) * chans, 2 * chans), BF16),
             vmem((pairs, nlon, 2 * chans), BF16),
             vmem((bands, pairs, 2, wide, chans), BF16),
@@ -510,12 +555,8 @@
             vmem((mb, degrees, 2 * fa), BF16),
             vmem((2 * chans, 2 * fa), BF16),
             vmem((4 * fields, 2 * chans), BF16),
-            vmem((members, fa, nlon), BF16),
             vmem((bands, wide, fa), BF16),
-            vmem((members * bands, wide, fa), BF16),
-            vmem((fa, nlon), F32),
             vmem((pl.cdiv(nlon, LANES), fa, LANES), F32),
-            vmem((fa, nlon), F32),
             dma((8,)),
             dma((4,)),
             dma((7,)),
@@ -527,7 +568,9 @@
             plain((1,)),
         ],
         compiler_params=pltpu.CompilerParams(
-            collective_id=0, has_side_effects=True, vmem_limit_bytes=60 * 1024 * 1024
+            collective_id=0,
+            has_side_effects=True,
+            vmem_limit_bytes=VMEM_BYTES - kept - 2 * 1024 * 1024,
         ),
     )(
         state,
@@ -539,7 +582,20 @@
         target,
         table,
     )
-    return out.reshape(1, fields, lat_rows, nlon)
+    tiles = pl.cdiv(nlon, LANES)
+    out = pl.pallas_call(
+        functools.partial(finish_kernel, members, bands),
+        out_shape=jax.ShapeDtypeStruct((fields, lat_rows, nlon), F32),
+        in_specs=[pl.BlockSpec(memory_space=pltpu.VMEM)] * 5,
+        out_specs=pl.BlockSpec(memory_space=pl.ANY),
+        scratch_shapes=[
+            vmem((tiles, fa, LANES), F32),
+            vmem((fields, lat_rows, nlon), F32),
+            dma((tiles,)),
+        ],
+        compiler_params=pltpu.CompilerParams(vmem_limit_bytes=16 * 1024 * 1024),
+    )(*arrived)
+    return out[None]
 
 
 def solution(mesh):

time: 28.1 us -> 28 us (level)
  local copies, waits for them, and re-layouts: 0.75 us -> 0 us
  Pallas kernels: 27.2 us -> 27.8 us
    unnamed x1 -> x0, local copies, waits for them, and re-layouts: 0.75 us -> none
    pallas_call x1 -> x2, Pallas kernels: 27.2 us -> 27.8 us  [the longest x1 26.7 us: local(): pl.pallas_call(functools.partial(kernel, members, bands), out_shape=resul...]
where the time goes in v4:
time: 28 us; the launch traced here: 27.8 us
  Pallas kernels  27.8 us (99%)
    pallas_call x1, Pallas kernels, local(): pl.pallas_call(functools.partial(kernel, members, bands), out_shape=resul...  26.7 us
    pallas_call x1, Pallas kernels, local(): pl.pallas_call(functools.partial(finish_kernel, members, bands), out_shap...  1.14 us

profile of v4, /device:TPU:0, one launch (start us, length us, event | category | flops | bytes accessed | tf_op | source)
XLA Modules:
  0.0 27.8 jit_solution(1072501341300755175)
XLA Ops:
  0.0 26.7 %shard_map.82 = (bf16[32,16,128]{2,1,0:T(8,128)(2,1)S(1)}, bf16[4,128,720]{2,1,0:T(8,128)(2,1)S(1)}, bf16[128,720]{1,0:T(8,128)(2,1)S(1)}, f32[128,720]{1,0:T(8,128)S(1)}, f32[128,720]{1,0:T(8,128)S(1)}) custom-call(bf16[1,8,720,128]{3,2,1,0:T(8,128)(2,1)} %state.1, bf16[9,128,128]{2,1,0:T(8,128)(2,1)} %conv_hbm.1, bf16[8,64,64]{2,1,0:T(8,128)(2,1)} %leg_hbm.1, ...), custom_call_target="tpu_custom_call" | custom-call | tf_op jit(solution)/shard_map/pallas_call | solution.py:532
  26.7 1.1 %shard_map.83 = f32[16,8,720]{2,1,0:T(8,128)} custom-call(bf16[32,16,128]{2,1,0:T(8,128)(2,1)S(1)} %get-tuple-element.10.everyone, bf16[4,128,720]{2,1,0:T(8,128)(2,1)S(1)} %get-tuple-element.11.directs, bf16[128,720]{1,0:T(8,128)(2,1)S(1)} %get-tuple-element.12.table, f32[128,720]{1,0:T(8,128)S(1)} %get-tuple-element.13.mine, ...), custom_call_target="tpu_custom_call" | custom-call | tf_op jit(solution)/shard_map/pallas_call | solution.py:586

commit v5 on v4

--- a/solution.py
+++ b/solution.py
@@ -55,6 +55,7 @@
     proj,
     target,
     toeplitz,
+    partial,
     mixed,
     spec,
     banded,
@@ -208,13 +209,19 @@
     def pair_of(t):
         return jnp.where(even, pairs - 1 - t, t)
 
-    def convolve(t):
-        p = pair_of(t)
-        window = [rows[2 * p + j] for j in range(2 * HALF + 2)]
-        conv = dot(jnp.concatenate(window, axis=1), toeplitz[...])
+    def mix(p, conv):
         own = jnp.concatenate([rows[2 * p + HALF], rows[2 * p + HALF + 1]], axis=1)
         half = conv * 0.5
         mixed[p] = (own.astype(F32) + half + half * jnp.tanh(half)).astype(BF16)
+
+    def window_sum(p, first, count):
+        window = [rows[2 * (p + first) + j] for j in range(2 * count)]
+        at = pl.ds(pl.multiple_of(first * 2 * chans, 2 * chans), count * 2 * chans)
+        return dot(jnp.concatenate(window, axis=1), toeplitz[at, :])
+
+    def convolve(t):
+        p = pair_of(t)
+        mix(p, window_sum(p, 0, HALF + 1))
 
     def transform(t):
         p = pair_of(t)
@@ -361,6 +368,9 @@
 
     send_spec(1, pairs - 2)
 
+    final_pair = pair_of(pairs - 1)
+    partial[...] = window_sum(final_pair, jnp.where(even, 1, 0), HALF)
+
     @pl.when(even)
     def _():
         halo_wait(True, 1)
@@ -369,7 +379,7 @@
     def _():
         halo_wait(False, 1)
 
-    convolve(pairs - 1)
+    mix(final_pair, partial[...] + window_sum(final_pair, jnp.where(even, 0, HALF), 1))
     transform(pairs - 1)
     send_spec(pairs - 1, pairs - 1)
     direct(pairs - 1)
@@ -418,26 +428,14 @@
             device_id=(member ^ k, s), device_id_type=MESH,
         ).start()
 
-    @pl.loop(1, bands)
-    def _(i):
-        dist = bands - i
-
-        @pl.when(band >= dist)
-        def _():
-            for k in range(members):
-                back(members - 1 - k, band - dist)
-
-    @pl.loop(1, bands)
-    def _(i):
-        dist = bands - i
-
-        @pl.when(band + dist < bands)
-        def _():
-            for k in range(members):
-                back(members - 1 - k, band + dist)
-
-    for k in range(1, members):
-        back(k, band)
+    for dest in range(members):
+
+        @pl.loop(0, bands)
+        def _(s):
+            @pl.when((s != band) | (member != dest))
+            def _():
+                back(member ^ dest, s)
+
     pltpu.make_async_copy(narrow.at[band], everyone.at[me], back_sems.at[member]).start()
 
     def back_wait(j):
@@ -543,6 +541,7 @@
             vmem((fields, chans), F32),
             vmem(target.shape, BF16),
             vmem(((2 * HALF + 2) * chans, 2 * chans), BF16),
+            vmem((nlon, 2 * chans), F32),
             vmem((pairs, nlon, 2 * chans), BF16),
             vmem((bands, pairs, 2, wide, chans), BF16),
             vmem((bands, pairs, 2, wide, chans), BF16),

time: 28 us -> 27.4 us (0.979)
  Pallas kernels: 27.8 us -> 27.2 us
    pallas_call x1, Pallas kernels: 26.7 us -> 26.1 us  [local(): pl.pallas_call(functools.partial(kernel, members, bands), out_shape=resul...]
where the time goes in v5:
time: 27.4 us; the launch traced here: 27.2 us
  Pallas kernels  27.2 us (99%)
    pallas_call x1, Pallas kernels, local(): pl.pallas_call(functools.partial(kernel, members, bands), out_shape=resul...  26.1 us
    pallas_call x1, Pallas kernels, local(): pl.pallas_call(functools.partial(finish_kernel, members, bands), out_shap...  1.14 us

profile of v5, /device:TPU:0, one launch (start us, length us, event | category | flops | bytes accessed | tf_op | source)
XLA Modules:
  0.0 27.2 jit_solution(161648657045444319)
XLA Ops:
  0.0 26.1 %shard_map.82 = (bf16[32,16,128]{2,1,0:T(8,128)(2,1)S(1)}, bf16[4,128,720]{2,1,0:T(8,128)(2,1)S(1)}, bf16[128,720]{1,0:T(8,128)(2,1)S(1)}, f32[128,720]{1,0:T(8,128)S(1)}, f32[128,720]{1,0:T(8,128)S(1)}) custom-call(bf16[1,8,720,128]{3,2,1,0:T(8,128)(2,1)} %state.1, bf16[9,128,128]{2,1,0:T(8,128)(2,1)} %conv_hbm.1, bf16[8,64,64]{2,1,0:T(8,128)(2,1)} %leg_hbm.1, ...), custom_call_target="tpu_custom_call" | custom-call | tf_op jit(solution)/shard_map/pallas_call | solution.py:530
  26.1 1.1 %shard_map.83 = f32[16,8,720]{2,1,0:T(8,128)} custom-call(bf16[32,16,128]{2,1,0:T(8,128)(2,1)S(1)} %get-tuple-element.10.everyone, bf16[4,128,720]{2,1,0:T(8,128)(2,1)S(1)} %get-tuple-element.11.directs, bf16[128,720]{1,0:T(8,128)(2,1)S(1)} %get-tuple-element.12.table, f32[128,720]{1,0:T(8,128)S(1)} %get-tuple-element.13.mine, ...), custom_call_target="tpu_custom_call" | custom-call | tf_op jit(solution)/shard_map/pallas_call | solution.py:585

commit v6 on v5

--- a/solution.py
+++ b/solution.py
@@ -60,7 +60,9 @@
     spec,
     banded,
     spread,
-    wtable,
+    wearly,
+    wlate,
+    early,
     leg_t,
     gather,
     masked,
@@ -326,7 +328,17 @@
 
     for i in (3, 4, 5, 7):
         loads[i].wait()
-    wtable[...] = (leg[...].astype(F32) * quad[...]).astype(BF16)
+    wtable = (leg[...].astype(F32) * quad[...]).astype(BF16).reshape(mb * degrees, nlat)
+    lat_at = lax.broadcasted_iota(jnp.int32, (nlat, nlat), 0)
+    place = lax.broadcasted_iota(jnp.int32, (nlat, nlat), 1)
+    source = place // 2 % bands
+    turn = place // (2 * bands)
+    pair_at = jnp.where(source % 2 == 0, pairs - 1 - turn, turn)
+    moved = lat_at == source * lat_rows + 2 * pair_at + place % 2
+    by_step = dot(wtable, jnp.where(moved, 1.0, 0.0).astype(BF16)).astype(BF16)
+    by_step = by_step.reshape(mb, degrees, nlat)
+    wearly[...] = by_step[:, :, : nlat - 2 * bands]
+    wlate[...] = by_step[:, :, nlat - 2 * bands :]
     for m in range(mb):
         leg_t[m] = leg[m].T
     r0 = lax.broadcasted_iota(jnp.int32, (wide, wide * lat_rows), 0)
@@ -384,23 +396,30 @@
     send_spec(pairs - 1, pairs - 1)
     direct(pairs - 1)
 
+    late = 2 * bands
+
     def spread_rows(t):
         for source in range(bands):
             q = pairs - 1 - t if source % 2 == 0 else t
-            at = (source * pairs + q) * 2 * wide
+            at = (t * bands + source) * 2 * wide
             spread[at : at + 2 * wide, :] = banded[source, q].astype(F32).reshape(2 * wide, chans)
+
+    def sums(m, weights, first, count):
+        re = spread[pl.ds(first * wide + m, count, stride=wide), :]
+        im = spread[pl.ds(first * wide + mb + m, count, stride=wide), :]
+        return dot(weights, jnp.concatenate([re, im], axis=1).astype(BF16))
 
     wait_spec(0, 0)
     wait_spec(1, pairs - 2)
     for t in range(pairs - 1):
         spread_rows(t)
+    for m in range(mb):
+        early[m] = sums(m, wearly[m], 0, nlat - late)
+    gain_re, gain_im = gain[0], gain[1]
     wait_spec(pairs - 1, pairs - 1)
     spread_rows(pairs - 1)
-    gain_re, gain_im = gain[0], gain[1]
     for m in range(mb):
-        re = spread[pl.ds(m, nlat, stride=wide), :]
-        im = spread[pl.ds(mb + m, nlat, stride=wide), :]
-        coef = dot(wtable[m], jnp.concatenate([re, im], axis=1).astype(BF16))
+        coef = early[m] + sums(m, wlate[m], nlat - late, late)
         c0, c1 = coef[:, :chans], coef[:, chans:]
         real, imag = c0 * gain_re - c1 * gain_im, c0 * gain_im + c1 * gain_re
         filt[m] = jnp.concatenate([real, imag], axis=1).astype(BF16)
@@ -489,7 +508,7 @@
     fa = fields * lat_rows
     k = everyone[pl.ds(last * bands, bands)].reshape(-1, fa).T
     copies = []
-    for i, start in enumerate(range(0, nlon, LANES)):
+    for i, start in enumerate(reversed(range(0, nlon, LANES))):
         width = min(LANES, nlon - start)
         at = slice(start, start + width)
         other = (directs[last, :, at].astype(F32) + dot(k, table[:, at])).astype(BF16)
@@ -546,7 +565,9 @@
             vmem((bands, pairs, 2, wide, chans), BF16),
             vmem((bands, pairs, 2, wide, chans), BF16),
             vmem((nlat * wide, chans), F32),
-            vmem(legendre.shape, BF16),
+            vmem((mb, degrees, nlat - 2 * bands), BF16),
+            vmem((mb, degrees, 2 * bands), BF16),
+            vmem((mb, degrees, 2 * chans), F32),
             vmem((mb, nlat, degrees), BF16),
             vmem((wide, wide * lat_rows), BF16),
             vmem((bands, wide, lat_rows, fa), BF16),

time: 27.4 us -> 27.3 us (level)
  no operation moved by 1% of the time
where the time goes in v6:
time: 27.3 us; the launch traced here: 27.2 us
  Pallas kernels  27.2 us (100%)
    pallas_call x1, Pallas kernels, local(): pl.pallas_call(functools.partial(kernel, members, bands), out_shape=resul...  26 us
    pallas_call x1, Pallas kernels, local(): pl.pallas_call(functools.partial(finish_kernel, members, bands), out_shap...  1.14 us

profile of v6, /device:TPU:0, one launch (start us, length us, event | category | flops | bytes accessed | tf_op | source)
XLA Modules:
  0.0 27.2 jit_solution(2484002719181036750)
XLA Ops:
  0.0 26.0 %shard_map.82 = (bf16[32,16,128]{2,1,0:T(8,128)(2,1)S(1)}, bf16[4,128,720]{2,1,0:T(8,128)(2,1)S(1)}, bf16[128,720]{1,0:T(8,128)(2,1)S(1)}, f32[128,720]{1,0:T(8,128)S(1)}, f32[128,720]{1,0:T(8,128)S(1)}) custom-call(bf16[1,8,720,128]{3,2,1,0:T(8,128)(2,1)} %state.1, bf16[9,128,128]{2,1,0:T(8,128)(2,1)} %conv_hbm.1, bf16[8,64,64]{2,1,0:T(8,128)(2,1)} %leg_hbm.1, ...), custom_call_target="tpu_custom_call" | custom-call | tf_op jit(solution)/shard_map/pallas_call | solution.py:549
  26.0 1.1 %shard_map.83 = f32[16,8,720]{2,1,0:T(8,128)} custom-call(bf16[32,16,128]{2,1,0:T(8,128)(2,1)S(1)} %get-tuple-element.10.everyone, bf16[4,128,720]{2,1,0:T(8,128)(2,1)S(1)} %get-tuple-element.11.directs, bf16[128,720]{1,0:T(8,128)(2,1)S(1)} %get-tuple-element.12.table, f32[128,720]{1,0:T(8,128)S(1)} %get-tuple-element.13.mine, ...), custom_call_target="tpu_custom_call" | custom-call | tf_op jit(solution)/shard_map/pallas_call | solution.py:606

commit v7 on v6

--- a/solution.py
+++ b/solution.py
@@ -195,9 +195,13 @@
         rows[HALF + lat_rows :] = jnp.zeros((HALF, nlon, chans), BF16)
 
     def halo_wait(low, far):
+        at = HALF - 2 - 2 * far if low else HALF + lat_rows + 2 * far
+        sem = 2 * (0 if low else 1) + far
+
         @pl.when(has_low if low else has_high)
         def _():
-            halo(low, far).wait_recv()
+            part = rows.at[pl.ds(at, 2)]
+            pltpu.make_async_copy(part, part, halo_sems.at[sem]).wait()
 
     loads[1].wait()
     taps = conv_w.shape[0]
@@ -530,6 +534,8 @@
     _, lat_rows, nlon, chans = state.shape
     mb, degrees, nlat = legendre.shape
     members, bands = lax.axis_size("member"), lax.axis_size("lat")
+    assert members & (members - 1) == 0 and bands % 2 == 0
+    assert lat_rows % 2 == 0 and lat_rows >= 6
     fields = project_weight.shape[1]
     fa, wide, pairs = fields * lat_rows, 2 * mb, lat_rows // 2
     table = dft_table(nlon, mb * bands, bands)

time: 27.3 us -> 27.3 us (level)
  no operation moved by 1% of the time
where the time goes in v7:
time: 27.3 us; the launch traced here: 27.2 us
  Pallas kernels  27.2 us (100%)
    pallas_call x1, Pallas kernels, local(): pl.pallas_call(functools.partial(kernel, members, bands), out_shape=resul...  26 us
    pallas_call x1, Pallas kernels, local(): pl.pallas_call(functools.partial(finish_kernel, members, bands), out_shap...  1.14 us

profile of v7, /device:TPU:0, one launch (start us, length us, event | category | flops | bytes accessed | tf_op | source)
XLA Modules:
  0.0 27.2 jit_solution(2484002719181036750)
XLA Ops:
  0.0 26.0 %shard_map.82 = (bf16[32,16,128]{2,1,0:T(8,128)(2,1)S(1)}, bf16[4,128,720]{2,1,0:T(8,128)(2,1)S(1)}, bf16[128,720]{1,0:T(8,128)(2,1)S(1)}, f32[128,720]{1,0:T(8,128)S(1)}, f32[128,720]{1,0:T(8,128)S(1)}) custom-call(bf16[1,8,720,128]{3,2,1,0:T(8,128)(2,1)} %state.1, bf16[9,128,128]{2,1,0:T(8,128)(2,1)} %conv_hbm.1, bf16[8,64,64]{2,1,0:T(8,128)(2,1)} %leg_hbm.1, ...), custom_call_target="tpu_custom_call" | custom-call | tf_op jit(solution)/shard_map/pallas_call | solution.py:555
  26.0 1.1 %shard_map.83 = f32[16,8,720]{2,1,0:T(8,128)} custom-call(bf16[32,16,128]{2,1,0:T(8,128)(2,1)S(1)} %get-tuple-element.10.everyone, bf16[4,128,720]{2,1,0:T(8,128)(2,1)S(1)} %get-tuple-element.11.directs, bf16[128,720]{1,0:T(8,128)(2,1)S(1)} %get-tuple-element.12.table, f32[128,720]{1,0:T(8,128)S(1)} %get-tuple-element.13.mine, ...), custom_call_target="tpu_custom_call" | custom-call | tf_op jit(solution)/shard_map/pallas_call | solution.py:612
